TPU v7x, 32 devices: a whole 2x2x4 slice. The times are simulated.
32 devices in a mesh: gx: 4 (over y, x), gy: 8 (over z, core).
Axes of the slice: x: 2, y: 2, z: 4, core: 2. Of those that a mesh axis runs over, the one named last changes fastest.
Arguments:
- velocity: float32 [3, 128, 64, 128], P(None, 'gx', 'gy'), may hold values from -6 to 6
- stress: float32 [6, 128, 64, 128], P(None, 'gx', 'gy'), may hold values from -6 to 6
- lame_first: float32 [128, 64, 128], P('gx', 'gy'), may hold values from 0.5 to 2
- modulus: float32 [128, 64, 128], P('gx', 'gy'), may hold values from 0.5 to 2
- buoyancy: float32 [128, 64, 128], P('gx', 'gy'), may hold values from 0.5 to 2
- zone: int32 [128, 64, 128], P('gx', 'gy'), may hold values from 0 to 7
- eligible: int32 [128, 64, 128], P('gx', 'gy'), may hold values 0 or 1
- cohesion: float32 [8], replicated, may hold values from 0.2 to 2
- friction: float32 [8], replicated, may hold values from 0.1 to 0.6
- source_cell: int32 [16], replicated, may hold values from 0 to 1048575
- source_moment: float32 [6, 16], replicated, may hold values from -15 to 15
Outputs:
- velocity_out: float32 [3, 128, 64, 128], P(None, 'gx', 'gy')
- stress_out: float32 [6, 128, 64, 128], P(None, 'gx', 'gy')
All inputs are finite; a program needn't handle non-finite values. No bound on the sum of `eligible` on one device may be relied on, other than what follows from the above.
Results may differ from a plain program's by a relative error of at most 0.00011.
Values sent between devices are 32-bit elements; how exact they have to be, the bound alone decides.
A program may use at most 64 MiB of HBM per device.

v0:
```python
import functools

import jax
import jax.numpy as jnp
from jax import lax
from jax.experimental import pallas as pl
from jax.experimental.pallas import tpu as pltpu
from jax.sharding import PartitionSpec as P

STEPS = 2
time_step = 0.1
shear_floor = 0.25
MESH = pl.DeviceIdType.MESH
CH = 8
R = 16

STRESS_X = ((0, 1, 2), (3, 2, 1), (4, 2, 1))
STRESS_Y = ((3, 2, 1), (1, 1, 2), (5, 2, 1))
FLOW_X = ((0, 2, 1), (1, 1, 2), (2, 1, 2))
FLOW_Y = ((0, 1, 2), (1, 2, 1), (2, 1, 2))
SPEC = {"s": (STRESS_X, STRESS_Y), "v": (FLOW_X, FLOW_Y)}


def kernel(
    nx,
    ny,
    vel_hbm, str_hbm, lam_hbm, mod_hbm, buo_hbm, zone_hbm, elig_hbm,
    coh_ref, fri_ref, cell_ref, moment_ref,
    vout_ref, sout_ref,
    xe, stage, vel, lam, mod, buo, zone, elig, inj, cc, cf,
    xb, yb, zb, pack_up, pack_dn, recv_up, recv_dn,
    load_sem, xsend, xrecv, ysend, yrecv,
):
    rows_x = lam.shape[0]
    rows_y = lam.shape[1]
    depth = lam.shape[2]
    chunks = rows_x // CH
    block = R * (rows_x + 1)
    phases = 2 * STEPS
    ix = lax.axis_index("gx")
    iy = lax.axis_index("gy")
    x_lo, x_hi, y_lo, y_hi = ix > 0, ix < nx - 1, iy > 0, iy < ny - 1

    barrier = pltpu.get_barrier_semaphore()
    sides = (
        (x_lo, (ix - 1, iy)),
        (x_hi, (ix + 1, iy)),
        (y_lo, (ix, iy - 1)),
        (y_hi, (ix, iy + 1)),
    )
    for there, target in sides:

        @pl.when(there)
        def _():
            pl.semaphore_signal(barrier, inc=1, device_id=target, device_id_type=MESH)

    loads = []

    def load(src, dst):
        copy = pltpu.make_async_copy(src, dst, load_sem.at[len(loads)])
        copy.start()
        loads.append(copy)

    for slot, (comp, low, high) in enumerate(STRESS_X):
        load(str_hbm.at[comp, pl.ds(rows_x - low, low)], xe.at[0, slot, pl.ds(0, low)])
        load(str_hbm.at[comp, pl.ds(0, high)], xe.at[1, slot, pl.ds(0, high)])
    edges, rest = len(loads), len(loads) + 3
    load(str_hbm.at[3], xb.at[0, 1, pl.ds(2, rows_x)])
    load(str_hbm.at[1], stage.at[0])
    load(str_hbm.at[5], stage.at[1])
    load(zone_hbm, zone)
    load(elig_hbm, elig)
    load(str_hbm.at[0], xb.at[0, 0, pl.ds(2, rows_x)])
    load(str_hbm.at[4], xb.at[0, 2, pl.ds(2, rows_x)])
    load(str_hbm.at[2], zb.at[0])
    load(vel_hbm, vel)
    load(buo_hbm, buo)
    late = len(loads)
    load(lam_hbm, lam)
    load(mod_hbm, mod)

    zero = jnp.zeros((rows_y, depth), jnp.float32)

    @pl.when(jnp.logical_not(x_lo))
    def _():
        for p in range(phases):
            for slot in range(3):
                for layer in (0, 1):
                    xb[p, slot, layer] = zero

    @pl.when(jnp.logical_not(x_hi))
    def _():
        for p in range(phases):
            for slot in range(3):
                for layer in (rows_x + 2, rows_x + 3):
                    xb[p, slot, layer] = zero

    @pl.when(jnp.logical_not(y_lo))
    def _():
        for p in range(phases):
            for c in range(chunks):
                recv_up[p, c] = jnp.zeros(recv_up.shape[2:], jnp.float32)

    @pl.when(jnp.logical_not(y_hi))
    def _():
        for p in range(phases):
            for c in range(chunks):
                recv_dn[p, c] = jnp.zeros(recv_dn.shape[2:], jnp.float32)

    def x_copy(p, slot, up):
        comp, low, high = SPEC["sv"[p % 2]][0][slot]
        if up:
            src = xe.at[0, slot, pl.ds(0, low)] if p == 0 else xb.at[p, slot, pl.ds(rows_x + 2 - low, low)]
            dst = xb.at[p, slot, pl.ds(2 - low, low)]
            target = (ix + 1, iy)
        else:
            src = xe.at[1, slot, pl.ds(0, high)] if p == 0 else xb.at[p, slot, pl.ds(2, high)]
            dst = xb.at[p, slot, pl.ds(rows_x + 2, high)]
            target = (ix - 1, iy)
        way = 0 if up else 1
        return pltpu.make_async_remote_copy(
            src_ref=src,
            dst_ref=dst,
            send_sem=xsend.at[p, way, slot],
            recv_sem=xrecv.at[p, way, slot],
            device_id=target,
            device_id_type=MESH,
        )

    def y_layers(p):
        spec = SPEC["sv"[p % 2]][1]
        up = [(slot, rows_y - low + i, i - low) for slot, (_, low, _) in enumerate(spec) for i in range(low)]
        dn = [(slot, i, rows_y + i) for slot, (_, _, high) in enumerate(spec) for i in range(high)]
        return up, dn

    def y_copy(p, c, up):
        rows = CH * len(y_layers(p)[0 if up else 1])
        packed, recv = (pack_up, recv_up) if up else (pack_dn, recv_dn)
        way = 0 if up else 1
        return pltpu.make_async_remote_copy(
            src_ref=packed.at[p, c, pl.ds(0, rows)],
            dst_ref=recv.at[p, c, pl.ds(0, rows)],
            send_sem=ysend.at[p, way, c],
            recv_sem=yrecv.at[p, way, c],
            device_id=(ix, iy + 1) if up else (ix, iy - 1),
            device_id_type=MESH,
        )

    def send_x(p, up):
        @pl.when(x_hi if up else x_lo)
        def _():
            for slot in range(3):
                x_copy(p, slot, up).start()

    def take_x(p, up):
        @pl.when(x_lo if up else x_hi)
        def _():
            for slot in range(3):
                x_copy(p, slot, up).wait_recv()

    def ybase(p, slot, x):
        return (p * 3 + slot) * block + R * (x + 1)

    def send_y(p, c):
        up, dn = y_layers(p)
        for layers, packed in ((up, pack_up), (dn, pack_dn)):
            for i, (slot, row, _) in enumerate(layers):
                start = ybase(p, slot, c * CH) + row
                packed[p, c, pl.ds(i * CH, CH), :] = yb[pl.ds(start, CH, stride=R), :]
        for there, way in ((y_hi, True), (y_lo, False)):

            @pl.when(there)
            def _():
                y_copy(p, c, way).start()

    def take_y(p, c):
        for there, way in ((y_lo, True), (y_hi, False)):

            @pl.when(there)
            def _():
                y_copy(p, c, way).wait_recv()

        up, dn = y_layers(p)
        for layers, recv in ((up, recv_up), (dn, recv_dn)):
            for i, (slot, _, row) in enumerate(layers):
                start = ybase(p, slot, c * CH) + row
                yb[pl.ds(start, CH, stride=R), :] = recv[p, c, pl.ds(i * CH, CH), :]

    order = [0] + ([chunks - 1] if chunks > 1 else []) + list(range(1, chunks - 1))

    for copy in loads[:edges]:
        copy.wait()

    def fill_y(c):
        def fill(i, carry):
            x = c * CH + i
            for slot, source in enumerate((None, 0, 1)):
                value = xb[0, 1, x + 2] if source is None else stage[source, x]
                yb[pl.ds(pl.multiple_of(ybase(0, slot, x), 8), rows_y), :] = value
            return carry

        lax.fori_loop(0, CH, fill, 0, unroll=True)

    heard = sum(there.astype(jnp.int32) for there, _ in sides)
    pl.semaphore_wait(barrier, heard)
    send_x(0, True)
    send_x(0, False)
    for copy in loads[edges:rest]:
        copy.wait()
    for c in order:
        fill_y(c)
        send_y(0, c)

    cell = cell_ref[...]
    bits = depth.bit_length() - 1
    assert depth == 1 << bits
    plane_row = cell >> bits
    cell_z = cell & (depth - 1)
    row = lax.broadcasted_iota(jnp.int32, (rows_x * rows_y, cell.shape[1]), 0)
    row_bits = rows_y.bit_length() - 1
    assert rows_y == 1 << row_bits
    row = (ix * rows_x + (row >> row_bits)) * (ny * rows_y) + iy * rows_y + (row & (rows_y - 1))
    match = row == plane_row
    at_z = (lax.broadcasted_iota(jnp.int32, (depth, cell.shape[1]), 0) == cell_z).astype(jnp.float32)
    for comp in range(6):
        moment = time_step * moment_ref[pl.ds(comp, 1), :]
        value = lax.dot_general(
            jnp.where(match, moment, 0.0),
            at_z,
            (((1,), (1,)), ((), ())),
            precision=lax.Precision.HIGHEST,
            preferred_element_type=jnp.float32,
        )
        inj[comp] = value.reshape(rows_x, rows_y, depth)

    for copy in loads[rest : rest + 2]:
        copy.wait()
    frictions, cohesions = [], []
    for which in range(coh_ref.shape[0]):
        f = jnp.full((rows_y, depth), fri_ref[which], jnp.float32)
        frictions.append(f)
        cohesions.append(coh_ref[which] * jnp.sqrt(1.0 - f * f))

    def table(x, carry):
        z = jnp.where(elig[x] == 1, zone[x], -1)
        c = jnp.full((rows_y, depth), 1e30, jnp.float32)
        f = jnp.zeros((rows_y, depth), jnp.float32)
        for which in range(coh_ref.shape[0]):
            hit = z == which
            c = jnp.where(hit, cohesions[which], c)
            f = jnp.where(hit, frictions[which], f)
        cc[x] = c
        cf[x] = f
        return carry

    lax.fori_loop(0, rows_x, table, 0, unroll=2)

    lane = lax.broadcasted_iota(jnp.int32, (rows_y, depth), 1)
    keep = {
        1: lane < depth - 1,
        2: lane < depth - 2,
        -1: lane >= 1,
        -2: lane >= 2,
    }

    def along_z(value, offset):
        if offset == 0:
            return value
        return jnp.where(keep[offset], pltpu.roll(value, (-offset) % depth, 1), 0.0)

    def derivative(get, forward):
        a, b, c, d = (get(1), get(0), get(2), get(-1)) if forward else (get(0), get(-1), get(1), get(-2))
        return 27.0 * (a - b) - (c - d)

    def dx(p, slot, x, forward):
        return derivative(lambda o: xb[p, slot, x + 2 + o], forward)

    def dy(p, slot, x, forward):
        return derivative(lambda o: yb[pl.ds(ybase(p, slot, x) + o, rows_y), :], forward)

    def dz(value, forward):
        return derivative(lambda o: along_z(value, o), forward)

    def put_y(p, slot, x, value):
        yb[pl.ds(pl.multiple_of(ybase(p, slot, x), 8), rows_y), :] = value

    def own_y(p, slot, x):
        return yb[pl.ds(pl.multiple_of(ybase(p, slot, x), 8), rows_y), :]

    def flow_layer(p, x):
        step = p // 2
        s = p
        scale = (time_step / 24.0) * buo[x]
        xz = xb[s, 2, x + 2]
        yz = own_y(s, 2, x)
        zz = zb[step, x]
        force_x = dx(s, 0, x, True) + dy(s, 0, x, False) + dz(xz, False)
        force_y = dx(s, 1, x, False) + dy(s, 1, x, True) + dz(yz, False)
        force_z = dx(s, 2, x, False) + dy(s, 2, x, False) + dz(zz, True)
        for slot, force in enumerate((force_x, force_y, force_z)):
            old = vel[slot, x] if step == 0 else xb[p - 1, slot, x + 2]
            new = old + scale * force
            xb[p + 1, slot, x + 2] = new
            put_y(p + 1, slot, x, new)
            if p == phases - 2:
                vout_ref[slot, x] = new

    def stress_layer(p, x):
        step = p // 2
        vx, vy, vz = (xb[p, slot, x + 2] for slot in range(3))
        ex = dx(p, 0, x, False)
        ey = dy(p, 1, x, False)
        ez = dz(vz, False)
        xy = dy(p, 0, x, True) + dx(p, 1, x, True)
        xz = dz(vx, True) + dx(p, 2, x, True)
        yz = dz(vy, True) + dy(p, 2, x, True)
        m = (time_step / 24.0) * mod[x]
        spread = (time_step / 24.0) * lam[x] * (ex + ey + ez)
        m2 = m + m
        s0, s3, s4 = (xb[p - 1, slot, x + 2] for slot in range(3))
        s1, s5 = own_y(p - 1, 1, x), own_y(p - 1, 2, x)
        s2 = zb[step, x]
        s0 = s0 + (spread + m2 * ex) + inj[0, x]
        s1 = s1 + (spread + m2 * ey) + inj[1, x]
        s2 = s2 + (spread + m2 * ez) + inj[2, x]
        s3 = s3 + m * xy + inj[3, x]
        s4 = s4 + m * xz + inj[4, x]
        s5 = s5 + m * yz + inj[5, x]
        pressure = (s0 + s1 + s2) * (1.0 / 3.0)
        d0, d1, d2 = s0 - pressure, s1 - pressure, s2 - pressure
        second = 0.5 * (d0 * d0 + d1 * d1 + d2 * d2) + (s3 * s3 + s4 * s4 + s5 * s5)
        strength = jnp.maximum(cc[x] - pressure * cf[x], 0.0)
        factor = jnp.minimum(1.0, strength * lax.rsqrt(jnp.maximum(second, shear_floor * shear_floor)))
        s0, s1, s2 = pressure + factor * d0, pressure + factor * d1, pressure + factor * d2
        s3, s4, s5 = factor * s3, factor * s4, factor * s5
        if p == phases - 1:
            for comp, value in enumerate((s0, s1, s2, s3, s4, s5)):
                sout_ref[comp, x] = value
            return
        for slot, value in enumerate((s0, s3, s4)):
            xb[p + 1, slot, x + 2] = value
        for slot, value in enumerate((s3, s1, s5)):
            put_y(p + 1, slot, x, value)
        zb[step + 1, x] = s2

    for p in range(phases):
        layer_of = flow_layer if p % 2 == 0 else stress_layer
        if p == 0:
            for copy in loads[rest + 2 : late]:
                copy.wait()
        elif p == 1:
            for copy in loads[late:]:
                copy.wait()
        for c in order:
            if c == 0:
                take_x(p, True)
            if c == chunks - 1:
                take_x(p, False)
            take_y(p, c)

            def one(i, carry, p=p, c=c, layer_of=layer_of):
                layer_of(p, c * CH + i)
                return carry

            lax.fori_loop(0, CH, one, 0, unroll=True)
            if p < phases - 1:
                if c == 0:
                    send_x(p + 1, False)
                if c == chunks - 1:
                    send_x(p + 1, True)
                send_y(p + 1, c)

    for p in range(phases):
        for there, way in ((x_hi, True), (x_lo, False)):

            @pl.when(there)
            def _():
                for slot in range(3):
                    x_copy(p, slot, way).wait_send()

        for there, way in ((y_hi, True), (y_lo, False)):

            @pl.when(there)
            def _():
                for c in range(chunks):
                    y_copy(p, c, way).wait_send()


def on_device(nx, ny, velocity, stress, lame_first, modulus, buoyancy, zone, eligible, cohesion, friction, source_cell, source_moment):
    rows_x, rows_y, depth = zone.shape
    assert rows_y <= 8 and rows_x % CH == 0
    chunks = rows_x // CH
    phases = 2 * STEPS
    f32 = jnp.float32
    grid = (rows_x, rows_y, depth)
    any_spec = pl.BlockSpec(memory_space=pltpu.HBM)
    smem = pl.BlockSpec(memory_space=pltpu.SMEM)
    vmem = pl.BlockSpec(memory_space=pltpu.VMEM)
    return pl.pallas_call(
        functools.partial(kernel, nx, ny),
        out_shape=(pltpu.VMEM((3,) + grid, f32), pltpu.VMEM((6,) + grid, f32)),
        in_specs=[any_spec] * 7 + [smem, smem, vmem, vmem],
        out_specs=(vmem, vmem),
        scratch_shapes=[
            pltpu.VMEM((2, 3, 2, rows_y, depth), f32),
            pltpu.VMEM((2,) + grid, f32),
            pltpu.VMEM((3,) + grid, f32),
            pltpu.VMEM(grid, f32),
            pltpu.VMEM(grid, f32),
            pltpu.VMEM(grid, f32),
            pltpu.VMEM(grid, jnp.int32),
            pltpu.VMEM(grid, jnp.int32),
            pltpu.VMEM((6,) + grid, f32),
            pltpu.VMEM(grid, f32),
            pltpu.VMEM(grid, f32),
            pltpu.VMEM((phases, 3, rows_x + 4, rows_y, depth), f32),
            pltpu.VMEM((phases * 3 * R * (rows_x + 1) + R, depth), f32),
            pltpu.VMEM((STEPS,) + grid, f32),
            pltpu.VMEM((phases, chunks, 5 * CH, depth), f32),
            pltpu.VMEM((phases, chunks, 5 * CH, depth), f32),
            pltpu.VMEM((phases, chunks, 5 * CH, depth), f32),
            pltpu.VMEM((phases, chunks, 5 * CH, depth), f32),
            pltpu.SemaphoreType.DMA((18,)),
            pltpu.SemaphoreType.DMA((phases, 2, 3)),
            pltpu.SemaphoreType.DMA((phases, 2, 3)),
            pltpu.SemaphoreType.DMA((phases, 2, chunks)),
            pltpu.SemaphoreType.DMA((phases, 2, chunks)),
        ],
        compiler_params=pltpu.CompilerParams(collective_id=0, has_side_effects=True),
    )(
        velocity, stress, lame_first, modulus, buoyancy, zone, eligible,
        cohesion, friction, source_cell.reshape(1, -1), source_moment,
    )


def solution(mesh):
    field = P(None, "gx", "gy", None)
    cells = P("gx", "gy", None)
    return jax.shard_map(
        functools.partial(on_device, mesh.shape["gx"], mesh.shape["gy"]),
        mesh=mesh,
        in_specs=(field, field, cells, cells, cells, cells, cells, P(), P(), P(), P()),
        out_specs=(field, field),
        check_vma=False,
    )
```

profile of v0, /device:TPU:21, one launch (start us, length us, event | category | flops | bytes accessed | tf_op | source)
XLA Modules:
  0.0 20.2 jit_solution(13629314534404950469)
XLA Ops:
  0.6 17.9 %shard_map.122 = (f32[3,32,8,128]{3,2,1,0:T(8,128)S(1)}, f32[6,32,8,128]{3,2,1,0:T(8,128)S(1)}) custom-call(f32[3,32,8,128]{3,2,1,0:T(8,128)} %vel_hbm.1, f32[6,32,8,128]{3,2,1,0:T(8,128)} %str_hbm.1, f32[32,8,128]{2,1,0:T(8,128)} %lam_hbm.1, f32[32,8,128]{2,1,0:T(8,128)} %mod_hbm.1, f32[32,8,128]{2,1,0:T(8,128)} %buo_hbm.1, s32[32,8,128]{2,1,0:T(8,128)} %zone_hbm.1, ...), custom_call_target="tpu_custom_call" | custom-call | tf_op jit(solution)/shard_map/pallas_call | solution.py:399
  18.5 0.7 %copy.15 = f32[3,32,8,128]{3,2,1,0:T(8,128)} copy(f32[3,32,8,128]{3,2,1,0:T(8,128)S(1)} %get-tuple-element.2) | data formatting | bytes 786432
  19.3 0.9 %copy.16 = f32[6,32,8,128]{3,2,1,0:T(8,128)} copy(f32[6,32,8,128]{3,2,1,0:T(8,128)S(1)} %get-tuple-element.3) | data formatting | bytes 1572864
where the time goes:
time: 20.4 us; the launch traced here: 20.2 us
  Pallas kernels  17.9 us (88%)
  local copies, waits for them, and re-layouts  1.63 us (8%)
  between operations  0.64 us (3%)
    pallas_call x1, Pallas kernels, on_device(): pl.pallas_call(functools.partial(kernel, nx, ny), out_shape=(pltpu.VMEM((...  17.9 us
    unnamed x2, local copies, waits for them, and re-layouts  1.63 us

commit v1 on v0

v1 whole, which is shorter than its diff:
```python
import functools

import jax
import jax.numpy as jnp
from jax import lax
from jax.experimental import pallas as pl
from jax.experimental.pallas import tpu as pltpu
from jax.sharding import PartitionSpec as P

STEPS = 2
time_step = 0.1
shear_floor = 0.25
MESH = pl.DeviceIdType.MESH
CH = 8
R = 16

BACK = {"F": 1, "B": 2}
AHEAD = {"F": 2, "B": 1}
FORCE_X = ((0, "F"), (3, "B"), (4, "B"))
FORCE_Y = ((3, "B"), (1, "F"), (5, "B"))
FLOW_X = ("B", "F", "F")
FLOW_Y = ("F", "B", "F")
SLOT_X = {0: 0, 3: 1, 4: 2}
SLOT_Y = {3: 0, 1: 1, 5: 2}


def edge(kind, up, n):
    return list(range(n - BACK[kind], n)) if up else list(range(AHEAD[kind]))


def spread(kind, up, n, get):
    if up and kind == "B":
        return [(0, get(0) - 27.0 * get(1)), (1, get(1))]
    if up:
        return [(0, get(0))]
    if kind == "B":
        return [(n - 1, -get(0))]
    return [(n - 1, 27.0 * get(0) - get(1)), (n - 2, -get(0))]


def raw_list(force, up, n):
    return [(comp, i) for comp, kind in force for i in edge(kind, up, n)]


def flow_list(flow, up, n):
    return [(slot, i) for slot, kind in enumerate(flow) for i in edge(kind, up, n)]


def corner_list(sx, sy, nx, ny):
    found = []
    for k in range(3):
        comp, kind = FORCE_Y[k]
        found += [(comp, x, y) for x in edge(FLOW_X[k], sx, nx) for y in edge(kind, sy, ny)]
        comp, kind = FORCE_X[k]
        found += [(comp, x, y) for x in edge(kind, sx, nx) for y in edge(FLOW_Y[k], sy, ny)]
    return list(dict.fromkeys(found))


CORNERS = [(True, True), (True, False), (False, True), (False, False)]


def kernel(
    nx,
    ny,
    vel_hbm, str_hbm, lam_hbm, mod_hbm, buo_hbm, zone_hbm, elig_hbm,
    coh_ref, fri_ref, cell_ref, moment_ref,
    vout_ref, sout_ref,
    stage, vel, lam, mod, buo, zone, elig, inj, cc, cf,
    sx, sy, zb, vb, xs, rx, ys, ry, ds, rd, xf, yf,
    load_sem, xsend, xrecv, ysend, yrecv, dsend, drecv,
):
    rows_x = lam.shape[0]
    rows_y = lam.shape[1]
    depth = lam.shape[2]
    chunks = rows_x // CH
    ix = lax.axis_index("gx")
    iy = lax.axis_index("gy")
    x_lo, x_hi, y_lo, y_hi = ix > 0, ix < nx - 1, iy > 0, iy < ny - 1

    def to_x(up):
        return (x_hi, (ix + 1, iy)) if up else (x_lo, (ix - 1, iy))

    def to_y(up):
        return (y_hi, (ix, iy + 1)) if up else (y_lo, (ix, iy - 1))

    def to_corner(cx, cy):
        there = jnp.logical_and(to_x(cx)[0], to_y(cy)[0])
        return there, (to_x(cx)[1][0], to_y(cy)[1][1])

    sides = [to_x(True), to_x(False), to_y(True), to_y(False)] + [to_corner(*c) for c in CORNERS]
    barrier = pltpu.get_barrier_semaphore()
    for there, target in sides:

        @pl.when(there)
        def _():
            pl.semaphore_signal(barrier, inc=1, device_id=target, device_id_type=MESH)

    raw_x = {up: raw_list(FORCE_X, up, rows_x) for up in (True, False)}
    raw_y = {up: raw_list(FORCE_Y, up, rows_y) for up in (True, False)}
    flow_x = {up: flow_list(FLOW_X, up, rows_x) for up in (True, False)}
    flow_y = {up: flow_list(FLOW_Y, up, rows_y) for up in (True, False)}
    buo_x = {True: [rows_x - 2, rows_x - 1], False: [0, 1]}
    buo_y = {True: [rows_y - 2, rows_y - 1], False: [0, 1]}
    corner = {c: corner_list(c[0], c[1], rows_x, rows_y) for c in CORNERS}

    loads = []

    def load(src, dst):
        copy = pltpu.make_async_copy(src, dst, load_sem.at[len(loads)])
        copy.start()
        loads.append(copy)

    def sx_row(step, comp, x):
        return ((step * 3 + SLOT_X[comp]) * (rows_x + 4) + x + 2) * rows_y

    def sy_row(step, comp, x):
        return (step * 3 + SLOT_Y[comp]) * R * (rows_x + 1) + R * (x + 1)

    def vb_row(step, slot, x):
        return ((step * 3 + slot) * (rows_x + 5) + x + 3) * R

    plane = rows_x * rows_y
    load(str_hbm.at[pl.ds(3 * plane, plane)], sx.at[pl.ds(sx_row(0, 3, 0), plane)])
    load(str_hbm.at[pl.ds(1 * plane, plane)], stage.at[0])
    load(str_hbm.at[pl.ds(5 * plane, plane)], stage.at[1])
    load(buo_hbm, buo)
    load(str_hbm.at[pl.ds(0 * plane, plane)], sx.at[pl.ds(sx_row(0, 0, 0), plane)])
    load(str_hbm.at[pl.ds(4 * plane, plane)], sx.at[pl.ds(sx_row(0, 4, 0), plane)])
    first = len(loads)
    load(str_hbm.at[pl.ds(2 * plane, plane)], zb.at[pl.ds(0, plane)])
    load(vel_hbm, vel)
    second = len(loads)
    load(zone_hbm, zone)
    load(elig_hbm, elig)
    third = len(loads)
    load(lam_hbm, lam)
    load(mod_hbm, mod)

    tile = jnp.zeros((rows_y, depth), jnp.float32)

    for step in range(STEPS):
        for comp in SLOT_X:
            for layer in (-2, -1, rows_x, rows_x + 1):
                sx[pl.ds(sx_row(step, comp, layer), rows_y), :] = tile
    for ref in (xf, yf):
        for i in range(ref.shape[0] // rows_y):
            ref[pl.ds(i * rows_y, rows_y), :] = tile

    def clear(i, carry):
        sy[pl.ds(pl.multiple_of(i * R + rows_y, 8), R - rows_y), :] = jnp.zeros((R - rows_y, depth), jnp.float32)
        return carry

    lax.fori_loop(0, sy.shape[0] // R, clear, 0, unroll=8)

    for up in (True, False):

        @pl.when(jnp.logical_not(to_x(not up)[0]))
        def _():
            for step in range(STEPS):
                for i in range(rx.shape[2]):
                    rx[step, int(up), i] = tile

        @pl.when(jnp.logical_not(to_y(not up)[0]))
        def _():
            for step in range(STEPS):

                def wipe(c, carry):
                    for i in range(ry.shape[3] // 8):
                        ry[step, int(up), c, pl.ds(i * 8, 8), :] = tile
                    return carry

                lax.fori_loop(0, chunks, wipe, 0)

    for d, (cx, cy) in enumerate(CORNERS):

        @pl.when(jnp.logical_not(to_corner(not cx, not cy)[0]))
        def _():
            for step in range(STEPS):
                for i in range(rd.shape[2] // 8):
                    rd[step, d, pl.ds(i * 8, 8), :] = tile

    def n_raw(raw, step):
        return len(raw) + (2 if step == 0 else 0)

    def x_copy(step, up, part):
        start, count = (0, n_raw(raw_x[up], step)) if part == 0 else (len(raw_x[up]) + 2, len(flow_x[up]))
        return pltpu.make_async_remote_copy(
            src_ref=xs.at[step, int(up), pl.ds(start, count)],
            dst_ref=rx.at[step, int(up), pl.ds(start, count)],
            send_sem=xsend.at[step, int(up), part],
            recv_sem=xrecv.at[step, int(up), part],
            device_id=to_x(up)[1],
            device_id_type=MESH,
        )

    def y_copy(step, up, c, part):
        start, count = (0, n_raw(raw_y[up], step)) if part == 0 else (len(raw_y[up]) + 2, len(flow_y[up]))
        return pltpu.make_async_remote_copy(
            src_ref=ys.at[step, int(up), c, pl.ds(start * 8, count * 8)],
            dst_ref=ry.at[step, int(up), c, pl.ds(start * 8, count * 8)],
            send_sem=ysend.at[step, int(up), c, part],
            recv_sem=yrecv.at[step, int(up), c, part],
            device_id=to_y(up)[1],
            device_id_type=MESH,
        )

    def d_copy(step, d):
        return pltpu.make_async_remote_copy(
            src_ref=ds.at[step, d],
            dst_ref=rd.at[step, d],
            send_sem=dsend.at[step, d],
            recv_sem=drecv.at[step, d],
            device_id=to_corner(*CORNERS[d])[1],
            device_id_type=MESH,
        )

    def sx_tile(step, comp, x):
        return sx[pl.ds(sx_row(step, comp, x), rows_y), :]

    def sy_pack(step, comp, c, row):
        return sy[pl.ds(sy_row(step, comp, c * CH) + row, CH, stride=R), :]

    def vb_pack(step, slot, c, row):
        return pl.ds(vb_row(step, slot, c * CH) + row, CH, stride=R)

    def pack_x_raw(step, up):
        for i, (comp, x) in enumerate(raw_x[up]):
            xs[step, int(up), i] = sx_tile(step, comp, x)
        if step == 0:
            for i, x in enumerate(buo_x[up]):
                xs[step, int(up), len(raw_x[up]) + i] = buo[pl.ds(x * rows_y, rows_y), :]

    def pack_y_raw(step, c):
        for up in (True, False):
            for i, (comp, row) in enumerate(raw_y[up]):
                ys[step, int(up), c, pl.ds(i * 8, 8), :] = sy_pack(step, comp, c, row)
            if step == 0:
                for i, row in enumerate(buo_y[up]):
                    value = buo[pl.ds(c * CH * rows_y + row, CH, stride=rows_y), :]
                    ys[step, int(up), c, pl.ds((len(raw_y[up]) + i) * 8, 8), :] = value

    def pack_x_flow(step, up):
        for i, (slot, x) in enumerate(flow_x[up]):
            xs[step, int(up), len(raw_x[up]) + 2 + i] = vb[pl.ds(vb_row(step, slot, x), rows_y), :]

    def pack_y_flow(step, c):
        for up in (True, False):
            for i, (slot, row) in enumerate(flow_y[up]):
                ys[step, int(up), c, pl.ds((len(raw_y[up]) + 2 + i) * 8, 8), :] = vb[vb_pack(step, slot, c, row), :]

    def pack_corners(step, cxs):
        for d, (cx, cy) in enumerate(CORNERS):
            if cx in cxs:
                for i, (comp, x, y) in enumerate(corner[(cx, cy)]):
                    if comp in SLOT_X:
                        value = sx[pl.ds(sx_row(step, comp, x) + y, 1), :]
                    else:
                        value = sy[pl.ds(sy_row(step, comp, x) + y, 1), :]
                    ds[step, d, pl.ds(i, 1), :] = value

    def send_x(step, up, parts):
        @pl.when(to_x(up)[0])
        def _():
            for part in parts:
                x_copy(step, up, part).start()

    def send_y(step, cs, parts):
        for up in (True, False):

            @pl.when(to_y(up)[0])
            def _():
                for c in cs:
                    for part in parts:
                        y_copy(step, up, c, part).start()

    def send_corners(step, cxs):
        for d, (cx, cy) in enumerate(CORNERS):
            if cx in cxs:

                @pl.when(to_corner(cx, cy)[0])
                def _():
                    d_copy(step, d).start()

    lane = lax.broadcasted_iota(jnp.int32, (rows_y, depth), 1)
    keep = {
        1: lane < depth - 1,
        2: lane < depth - 2,
        -1: lane >= 1,
        -2: lane >= 2,
    }

    def along_z(value, offset):
        if offset == 0:
            return value
        return jnp.where(keep[offset], pltpu.roll(value, (-offset) % depth, 1), 0.0)

    def derivative(get, forward):
        a, b, c, d = (get(1), get(0), get(2), get(-1)) if forward else (get(0), get(-1), get(1), get(-2))
        return 27.0 * (a - b) - (c - d)

    def s_dx(step, comp, x, forward):
        return derivative(lambda o: sx_tile(step, comp, x + o), forward)

    def s_dy(step, comp, x, forward):
        return derivative(lambda o: sy[pl.ds(sy_row(step, comp, x) + o, rows_y), :], forward)

    def v_dx(step, slot, x, forward):
        return derivative(lambda o: vb[pl.ds(vb_row(step, slot, x + o), rows_y), :], forward)

    def v_dy(step, slot, x, forward):
        return derivative(lambda o: vb[pl.ds(vb_row(step, slot, x) + o, rows_y), :], forward)

    def dz(value, forward):
        return derivative(lambda o: along_z(value, o), forward)

    def own_sy(step, comp, x):
        return sy[pl.ds(sy_row(step, comp, x), rows_y), :]

    def own_zb(step, x):
        return zb[pl.ds((step * rows_x + x) * rows_y, rows_y), :]

    def own_v(step, slot, x):
        return vb[pl.ds(vb_row(step, slot, x), rows_y), :]

    def of_cell(ref, x):
        return ref[pl.ds(x * rows_y, rows_y), :]

    weight = time_step / 24.0

    def flow_layer(step, x):
        scale = weight * of_cell(buo, x)
        xz = sx_tile(step, 4, x)
        yz = own_sy(step, 5, x)
        zz = own_zb(step, x)
        force_x = s_dx(step, 0, x, True) + s_dy(step, 3, x, False) + dz(xz, False)
        force_y = s_dx(step, 3, x, False) + s_dy(step, 1, x, True) + dz(yz, False)
        force_z = s_dx(step, 4, x, False) + s_dy(step, 5, x, False) + dz(zz, True)
        for slot, force in enumerate((force_x, force_y, force_z)):
            old = vel[pl.ds((slot * rows_x + x) * rows_y, rows_y), :] if step == 0 else own_v(step - 1, slot, x)
            vb[pl.ds(vb_row(step, slot, x), rows_y), :] = old + scale * force

    def wait_x(step):
        for up in (True, False):

            @pl.when(to_x(not up)[0])
            def _():
                for part in (0, 1):
                    x_copy(step, up, part).wait_recv()

    def wait_y(step):
        for up in (True, False):

            @pl.when(to_y(not up)[0])
            def _():
                for c in range(chunks):
                    for part in (0, 1):
                        y_copy(step, up, c, part).wait_recv()

    def wait_corners(step):
        for d, (cx, cy) in enumerate(CORNERS):

            @pl.when(to_corner(not cx, not cy)[0])
            def _():
                d_copy(step, d).wait_recv()

    def place(items, what):
        return [i for i, item in enumerate(items) if item == what][0]

    def take_corners(step):
        for d, (cx, cy) in enumerate(CORNERS):

            def raw(comp, x, y):
                return rd[step, d, pl.ds(place(corner[(cx, cy)], (comp, x, y)), 1), :]

            for k in range(3):
                comp, kind = FORCE_Y[k]
                ys_ = edge(kind, cy, rows_y)
                for x in edge(FLOW_X[k], cx, rows_x):
                    base = (int(cx) * 5 + place(flow_x[cx], (k, x))) * rows_y
                    for row, value in spread(kind, cy, rows_y, lambda i: raw(comp, x, ys_[i])):
                        xf[pl.ds(base + row, 1), :] = value
                comp, kind = FORCE_X[k]
                xs_ = edge(kind, cx, rows_x)
                for y in edge(FLOW_Y[k], cy, rows_y):
                    base = ((int(cy) * 5 + place(flow_y[cy], (k, y))) * 2 + int(cx)) * 8
                    for layer, value in spread(kind, cx, CH, lambda i: raw(comp, xs_[i], y)):
                        yf[pl.ds(base + layer, 1), :] = value

    def finish_x(step):
        for up in (True, False):
            side = int(up)
            for k, (comp, kind) in enumerate(FORCE_X):
                places = [place(raw_x[up], (comp, x)) for x in edge(kind, up, rows_x)]
                for x, value in spread(kind, up, rows_x, lambda i: rx[step, side, places[i]]):
                    where = pl.ds(vb_row(step, k, x), rows_y)
                    vb[where, :] = vb[where, :] + weight * of_cell(buo, x) * value
            for k, (comp, kind) in enumerate(FORCE_X):
                mine = edge(kind, not up, rows_x)
                adds = dict(spread(kind, not up, rows_x, lambda i: sx_tile(step, comp, mine[i])))
                for x in edge(FLOW_X[k], up, rows_x):
                    i = place(flow_x[up], (k, x))
                    add = adds[x] + xf[pl.ds((side * 5 + i) * rows_y, rows_y), :]
                    scale = weight * rx[0, side, len(raw_x[up]) + place(buo_x[up], x)]
                    new = rx[step, side, len(raw_x[up]) + 2 + i] + scale * add
                    at = x - rows_x if up else x + rows_x
                    vb[pl.ds(vb_row(step, k, at), rows_y), :] = new

    def finish_y(step, c):
        for up in (True, False):
            side = int(up)

            def got(i):
                return ry[step, side, c, pl.ds(i * 8, 8), :]

            for k, (comp, kind) in enumerate(FORCE_Y):
                places = [place(raw_y[up], (comp, y)) for y in edge(kind, up, rows_y)]
                for y, value in spread(kind, up, rows_y, lambda i: got(places[i])):
                    where = vb_pack(step, k, c, y)
                    scale = weight * buo[pl.ds(c * CH * rows_y + y, CH, stride=rows_y), :]
                    vb[where, :] = vb[where, :] + scale * value
            for k, (comp, kind) in enumerate(FORCE_Y):
                mine = edge(kind, not up, rows_y)
                adds = dict(spread(kind, not up, rows_y, lambda i: sy_pack(step, comp, c, mine[i])))
                for y in edge(FLOW_Y[k], up, rows_y):
                    i = place(flow_y[up], (k, y))
                    add = adds[y]
                    for end, at_end in ((1, 0), (0, chunks - 1)):
                        if c == at_end:
                            add = add + yf[pl.ds(((side * 5 + i) * 2 + end) * 8, 8), :]
                    scale = weight * ry[0, side, c, pl.ds((len(raw_y[up]) + place(buo_y[up], y)) * 8, 8), :]
                    new = got(len(raw_y[up]) + 2 + i) + scale * add
                    at = y - rows_y if up else y + rows_y
                    vb[vb_pack(step, k, c, at), :] = new

    def stress_layer(step, x):
        last = step == STEPS - 1
        vx, vy, vz = (own_v(step, slot, x) for slot in range(3))
        if last:
            for slot, value in enumerate((vx, vy, vz)):
                vout_ref[slot, x] = value
        ex = v_dx(step, 0, x, False)
        ey = v_dy(step, 1, x, False)
        ez = dz(vz, False)
        xy = v_dy(step, 0, x, True) + v_dx(step, 1, x, True)
        xz = dz(vx, True) + v_dx(step, 2, x, True)
        yz = dz(vy, True) + v_dy(step, 2, x, True)
        m = weight * mod[x]
        grow = weight * lam[x] * (ex + ey + ez)
        m2 = m + m
        s0, s3, s4 = (sx_tile(step, comp, x) for comp in (0, 3, 4))
        s1, s5 = own_sy(step, 1, x), own_sy(step, 5, x)
        s2 = own_zb(step, x)
        s0 = s0 + (grow + m2 * ex) + inj[0, x]
        s1 = s1 + (grow + m2 * ey) + inj[1, x]
        s2 = s2 + (grow + m2 * ez) + inj[2, x]
        s3 = s3 + m * xy + inj[3, x]
        s4 = s4 + m * xz + inj[4, x]
        s5 = s5 + m * yz + inj[5, x]
        pressure = (s0 + s1 + s2) * (1.0 / 3.0)
        d0, d1, d2 = s0 - pressure, s1 - pressure, s2 - pressure
        second = 0.5 * (d0 * d0 + d1 * d1 + d2 * d2) + (s3 * s3 + s4 * s4 + s5 * s5)
        strength = jnp.maximum(cc[x] - pressure * cf[x], 0.0)
        factor = jnp.minimum(1.0, strength * lax.rsqrt(jnp.maximum(second, shear_floor * shear_floor)))
        s0, s1, s2 = pressure + factor * d0, pressure + factor * d1, pressure + factor * d2
        s3, s4, s5 = factor * s3, factor * s4, factor * s5
        if last:
            for comp, value in enumerate((s0, s1, s2, s3, s4, s5)):
                sout_ref[comp, x] = value
            return
        for comp, value in ((0, s0), (3, s3), (4, s4)):
            sx[pl.ds(sx_row(step + 1, comp, x), rows_y), :] = value
        for comp, value in ((3, s3), (1, s1), (5, s5)):
            sy[pl.ds(sy_row(step + 1, comp, x), rows_y), :] = value
        zb[pl.ds(((step + 1) * rows_x + x) * rows_y, rows_y), :] = s2

    for copy in loads[:first]:
        copy.wait()

    def fill_y(i, carry):
        at = pl.multiple_of(i * rows_y, 8)
        for comp, value in (
            (3, sx[pl.ds(sx_row(0, 3, 0) + at, rows_y), :]),
            (1, stage[0, pl.ds(at, rows_y), :]),
            (5, stage[1, pl.ds(at, rows_y), :]),
        ):
            sy[pl.ds(pl.multiple_of(sy_row(0, comp, 0) + i * R, 8), rows_y), :] = value
        return carry

    lax.fori_loop(0, rows_x, fill_y, 0, unroll=8)
    for up in (True, False):
        pack_x_raw(0, up)
    pack_corners(0, (True, False))
    for c in range(chunks):
        pack_y_raw(0, c)
    heard = sum(there.astype(jnp.int32) for there, _ in sides)
    pl.semaphore_wait(barrier, heard)
    for up in (True, False):
        send_x(0, up, (0,))
    send_corners(0, (True, False))
    send_y(0, range(chunks), (0,))
    for copy in loads[first:second]:
        copy.wait()
    order = [0] + ([chunks - 1] if chunks > 1 else []) + list(range(1, chunks - 1))
    for c in order:
        for i in range(CH):
            flow_layer(0, c * CH + i)
        if c == 0:
            pack_x_flow(0, False)
            send_x(0, False, (1,))
        if c == chunks - 1:
            pack_x_flow(0, True)
            send_x(0, True, (1,))
        pack_y_flow(0, c)
        send_y(0, (c,), (1,))

    cell = cell_ref[...]
    bits = depth.bit_length() - 1
    assert depth == 1 << bits
    plane_row = cell >> bits
    cell_z = cell & (depth - 1)
    row = lax.broadcasted_iota(jnp.int32, (rows_x * rows_y, cell.shape[1]), 0)
    row_bits = rows_y.bit_length() - 1
    assert rows_y == 1 << row_bits
    row = (ix * rows_x + (row >> row_bits)) * (ny * rows_y) + iy * rows_y + (row & (rows_y - 1))
    match = row == plane_row
    at_z = (lax.broadcasted_iota(jnp.int32, (depth, cell.shape[1]), 0) == cell_z).astype(jnp.float32)
    for comp in range(6):
        moment = time_step * moment_ref[pl.ds(comp, 1), :]
        value = lax.dot_general(
            jnp.where(match, moment, 0.0),
            at_z,
            (((1,), (1,)), ((), ())),
            precision=lax.Precision.HIGHEST,
            preferred_element_type=jnp.float32,
        )
        inj[comp] = value.reshape(rows_x, rows_y, depth)

    for copy in loads[second:third]:
        copy.wait()
    frictions, cohesions = [], []
    for which in range(coh_ref.shape[0]):
        f = jnp.full((rows_y, depth), fri_ref[which], jnp.float32)
        frictions.append(f)
        cohesions.append(coh_ref[which] * jnp.sqrt(1.0 - f * f))

    def table(x, carry):
        z = jnp.where(elig[x] == 1, zone[x], -1)
        c = jnp.full((rows_y, depth), 1e30, jnp.float32)
        f = jnp.zeros((rows_y, depth), jnp.float32)
        for which in range(coh_ref.shape[0]):
            hit = z == which
            c = jnp.where(hit, cohesions[which], c)
            f = jnp.where(hit, frictions[which], f)
        cc[x] = c
        cf[x] = f
        return carry

    lax.fori_loop(0, rows_x, table, 0, unroll=2)

    for copy in loads[third:]:
        copy.wait()

    for step in range(STEPS):
        wait_corners(step)
        take_corners(step)
        wait_x(step)
        finish_x(step)
        wait_y(step)
        for c in range(chunks):
            finish_y(step, c)
        last = step == STEPS - 1
        done = 0
        stressed = set()
        flowed = set()
        sent = set()
        for c in order:
            for i in range(CH):
                stress_layer(step, c * CH + i)
            if last:
                continue
            nxt = step + 1
            stressed.update(range(c * CH, (c + 1) * CH))
            pack_y_raw(nxt, c)
            send_y(nxt, (c,), (0,))
            if c == 0:
                pack_corners(nxt, (False,))
                send_corners(nxt, (False,))
                pack_x_raw(nxt, False)
            if c == chunks - 1:
                pack_corners(nxt, (True,))
                send_corners(nxt, (True,))
                pack_x_raw(nxt, True)
            for x in range(rows_x):
                near = range(max(x - 2, 0), min(x + 3, rows_x))
                if x not in flowed and all(n in stressed for n in near):
                    flow_layer(nxt, x)
                    flowed.add(x)
            if c == 0:
                pack_x_flow(nxt, False)
                send_x(nxt, False, (0, 1))
            if c == chunks - 1:
                pack_x_flow(nxt, True)
                send_x(nxt, True, (0, 1))
            for other in order:
                if other not in sent and all(x in flowed for x in range(other * CH, (other + 1) * CH)):
                    pack_y_flow(nxt, other)
                    send_y(nxt, (other,), (1,))
                    sent.add(other)

    for step in range(STEPS):
        for up in (True, False):

            @pl.when(to_x(up)[0])
            def _():
                for part in (0, 1):
                    x_copy(step, up, part).wait_send()

            @pl.when(to_y(up)[0])
            def _():
                for c in range(chunks):
                    for part in (0, 1):
                        y_copy(step, up, c, part).wait_send()

        for d, (cx, cy) in enumerate(CORNERS):

            @pl.when(to_corner(cx, cy)[0])
            def _():
                d_copy(step, d).wait_send()


def on_device(nx, ny, velocity, stress, lame_first, modulus, buoyancy, zone, eligible, cohesion, friction, source_cell, source_moment):
    rows_x, rows_y, depth = zone.shape
    assert rows_y == 8 and rows_x % CH == 0
    chunks = rows_x // CH
    f32 = jnp.float32
    grid = (rows_x, rows_y, depth)
    plane = rows_x * rows_y
    any_spec = pl.BlockSpec(memory_space=pltpu.HBM)
    smem = pl.BlockSpec(memory_space=pltpu.SMEM)
    vmem = pl.BlockSpec(memory_space=pltpu.VMEM)
    dma = pltpu.SemaphoreType.DMA
    return pl.pallas_call(
        functools.partial(kernel, nx, ny),
        out_shape=(pltpu.VMEM((3,) + grid, f32), pltpu.VMEM((6,) + grid, f32)),
        in_specs=[any_spec] * 7 + [smem, smem, vmem, vmem],
        out_specs=(vmem, vmem),
        scratch_shapes=[
            pltpu.VMEM((2, plane, depth), f32),
            pltpu.VMEM((3 * plane, depth), f32),
            pltpu.VMEM(grid, f32),
            pltpu.VMEM(grid, f32),
            pltpu.VMEM((plane, depth), f32),
            pltpu.VMEM(grid, jnp.int32),
            pltpu.VMEM(grid, jnp.int32),
            pltpu.VMEM((6,) + grid, f32),
            pltpu.VMEM(grid, f32),
            pltpu.VMEM(grid, f32),
            pltpu.VMEM((STEPS * 3 * (rows_x + 4) * rows_y, depth), f32),
            pltpu.VMEM((STEPS * 3 * R * (rows_x + 1) + R, depth), f32),
            pltpu.VMEM((STEPS * plane, depth), f32),
            pltpu.VMEM((STEPS * 3 * (rows_x + 5) * R, depth), f32),
            pltpu.VMEM((STEPS, 2, 11, rows_y, depth), f32),
            pltpu.VMEM((STEPS, 2, 11, rows_y, depth), f32),
            pltpu.VMEM((STEPS, 2, chunks, 11 * 8, depth), f32),
            pltpu.VMEM((STEPS, 2, chunks, 11 * 8, depth), f32),
            pltpu.VMEM((STEPS, 4, 16, depth), f32),
            pltpu.VMEM((STEPS, 4, 16, depth), f32),
            pltpu.VMEM((2 * 5 * rows_y, depth), f32),
            pltpu.VMEM((2 * 5 * 2 * 8, depth), f32),
            dma((12,)),
            dma((STEPS, 2, 2)),
            dma((STEPS, 2, 2)),
            dma((STEPS, 2, chunks, 2)),
            dma((STEPS, 2, chunks, 2)),
            dma((STEPS, 4)),
            dma((STEPS, 4)),
        ],
        compiler_params=pltpu.CompilerParams(collective_id=0, has_side_effects=True),
    )(
        velocity.reshape(3 * plane, depth), stress.reshape(6 * plane, depth), lame_first, modulus,
        buoyancy.reshape(plane, depth), zone, eligible,
        cohesion, friction, source_cell.reshape(1, -1), source_moment,
    )


def solution(mesh):
    field = P(None, "gx", "gy", None)
    cells = P("gx", "gy", None)
    return jax.shard_map(
        functools.partial(on_device, mesh.shape["gx"], mesh.shape["gy"]),
        mesh=mesh,
        in_specs=(field, field, cells, cells, cells, cells, cells, P(), P(), P(), P()),
        out_specs=(field, field),
        check_vma=False,
    )
```

time: 20.4 us -> 17.9 us (0.88)
  the two profiles are of different devices: /device:TPU:21 before, /device:TPU:1 now
where the time goes in v1:
time: 17.9 us; the launch traced here: 17.7 us
  Pallas kernels  15.4 us (86%)
  local copies, waits for them, and re-layouts  1.63 us (9%)
  between operations  0.64 us (4%)
    pallas_call x1, Pallas kernels, on_device(): pl.pallas_call(functools.partial(kernel, nx, ny), out_shape=(pltpu.VMEM((...  15.4 us
    unnamed x2, local copies, waits for them, and re-layouts  1.63 us

profile of v1, /device:TPU:1, one launch (start us, length us, event | category | flops | bytes accessed | tf_op | source)
XLA Modules:
  0.0 17.7 jit_solution(6214769251460126691)
XLA Ops:
  0.6 15.4 %shard_map.122 = (f32[3,32,8,128]{3,2,1,0:T(8,128)S(1)}, f32[6,32,8,128]{3,2,1,0:T(8,128)S(1)}) custom-call(f32[768,128]{1,0:T(8,128)} %bitcast.5, f32[1536,128]{1,0:T(8,128)} %bitcast.4, f32[32,8,128]{2,1,0:T(8,128)} %lam_hbm.1, f32[32,8,128]{2,1,0:T(8,128)} %mod_hbm.1, f32[256,128]{1,0:T(8,128)} %bitcast.6, s32[32,8,128]{2,1,0:T(8,128)} %zone_hbm.1, ...), custom_call_target="tpu_custom_call" | custom-call | tf_op jit(solution)/shard_map/pallas_call | solution.py:642
  16.1 0.7 %copy.15 = f32[3,32,8,128]{3,2,1,0:T(8,128)} copy(f32[3,32,8,128]{3,2,1,0:T(8,128)S(1)} %get-tuple-element.2) | data formatting | bytes 786432
  16.8 0.9 %copy.16 = f32[6,32,8,128]{3,2,1,0:T(8,128)} copy(f32[6,32,8,128]{3,2,1,0:T(8,128)S(1)} %get-tuple-element.3) | data formatting | bytes 1572864

commit v2 on v1

--- a/solution.py
+++ b/solution.py
@@ -179,22 +179,23 @@
                 for i in range(rd.shape[2] // 8):
                     rd[step, d, pl.ds(i * 8, 8), :] = tile
 
-    def n_raw(raw, step):
-        return len(raw) + (2 if step == 0 else 0)
-
-    def x_copy(step, up, part):
-        start, count = (0, n_raw(raw_x[up], step)) if part == 0 else (len(raw_x[up]) + 2, len(flow_x[up]))
+    def x_copy(step, up):
+        count = len(raw_x[up]) + len(flow_x[up]) + (2 if step == 0 else 0)
         return pltpu.make_async_remote_copy(
-            src_ref=xs.at[step, int(up), pl.ds(start, count)],
-            dst_ref=rx.at[step, int(up), pl.ds(start, count)],
-            send_sem=xsend.at[step, int(up), part],
-            recv_sem=xrecv.at[step, int(up), part],
+            src_ref=xs.at[step, int(up), pl.ds(0, count)],
+            dst_ref=rx.at[step, int(up), pl.ds(0, count)],
+            send_sem=xsend.at[step, int(up)],
+            recv_sem=xrecv.at[step, int(up)],
             device_id=to_x(up)[1],
             device_id_type=MESH,
         )
 
+    def y_parts(step):
+        return (0,) if step == 0 else (0, 1)
+
     def y_copy(step, up, c, part):
-        start, count = (0, n_raw(raw_y[up], step)) if part == 0 else (len(raw_y[up]) + 2, len(flow_y[up]))
+        raw, flow = len(raw_y[up]), len(flow_y[up])
+        start, count = (0, raw + flow + 2) if step == 0 else ((0, raw), (raw, flow))[part]
         return pltpu.make_async_remote_copy(
             src_ref=ys.at[step, int(up), c, pl.ds(start * 8, count * 8)],
             dst_ref=ry.at[step, int(up), c, pl.ds(start * 8, count * 8)],
@@ -206,8 +207,8 @@
 
     def d_copy(step, d):
         return pltpu.make_async_remote_copy(
-            src_ref=ds.at[step, d],
-            dst_ref=rd.at[step, d],
+            src_ref=ds.at[step, d, pl.ds(0, len(corner[CORNERS[d]]))],
+            dst_ref=rd.at[step, d, pl.ds(0, len(corner[CORNERS[d]]))],
             send_sem=dsend.at[step, d],
             recv_sem=drecv.at[step, d],
             device_id=to_corner(*CORNERS[d])[1],
@@ -228,7 +229,7 @@
             xs[step, int(up), i] = sx_tile(step, comp, x)
         if step == 0:
             for i, x in enumerate(buo_x[up]):
-                xs[step, int(up), len(raw_x[up]) + i] = buo[pl.ds(x * rows_y, rows_y), :]
+                xs[step, int(up), len(raw_x[up]) + len(flow_x[up]) + i] = buo[pl.ds(x * rows_y, rows_y), :]
 
     def pack_y_raw(step, c):
         for up in (True, False):
@@ -237,16 +238,16 @@
             if step == 0:
                 for i, row in enumerate(buo_y[up]):
                     value = buo[pl.ds(c * CH * rows_y + row, CH, stride=rows_y), :]
-                    ys[step, int(up), c, pl.ds((len(raw_y[up]) + i) * 8, 8), :] = value
+                    ys[step, int(up), c, pl.ds((len(raw_y[up]) + len(flow_y[up]) + i) * 8, 8), :] = value
 
     def pack_x_flow(step, up):
         for i, (slot, x) in enumerate(flow_x[up]):
-            xs[step, int(up), len(raw_x[up]) + 2 + i] = vb[pl.ds(vb_row(step, slot, x), rows_y), :]
+            xs[step, int(up), len(raw_x[up]) + i] = vb[pl.ds(vb_row(step, slot, x), rows_y), :]
 
     def pack_y_flow(step, c):
         for up in (True, False):
             for i, (slot, row) in enumerate(flow_y[up]):
-                ys[step, int(up), c, pl.ds((len(raw_y[up]) + 2 + i) * 8, 8), :] = vb[vb_pack(step, slot, c, row), :]
+                ys[step, int(up), c, pl.ds((len(raw_y[up]) + i) * 8, 8), :] = vb[vb_pack(step, slot, c, row), :]
 
     def pack_corners(step, cxs):
         for d, (cx, cy) in enumerate(CORNERS):
@@ -258,11 +259,14 @@
                         value = sy[pl.ds(sy_row(step, comp, x) + y, 1), :]
                     ds[step, d, pl.ds(i, 1), :] = value
 
-    def send_x(step, up, parts):
-        @pl.when(to_x(up)[0])
-        def _():
-            for part in parts:
-                x_copy(step, up, part).start()
+    def send_x(step, core):
+        mine = iy % 2 == core
+        odd = ix % 2 == 1
+        for up, when in ((True, odd), (False, True), (True, jnp.logical_not(odd))):
+
+            @pl.when(jnp.logical_and(jnp.logical_and(to_x(up)[0], mine), when))
+            def _():
+                x_copy(step, up).start()
 
     def send_y(step, cs, parts):
         for up in (True, False):
@@ -344,16 +348,15 @@
 
             @pl.when(to_x(not up)[0])
             def _():
-                for part in (0, 1):
-                    x_copy(step, up, part).wait_recv()
-
-    def wait_y(step):
+                x_copy(step, up).wait_recv()
+
+    def wait_y(step, cs):
         for up in (True, False):
 
             @pl.when(to_y(not up)[0])
             def _():
-                for c in range(chunks):
-                    for part in (0, 1):
+                for c in cs:
+                    for part in y_parts(step):
                         y_copy(step, up, c, part).wait_recv()
 
     def wait_corners(step):
@@ -400,10 +403,14 @@
                 for x in edge(FLOW_X[k], up, rows_x):
                     i = place(flow_x[up], (k, x))
                     add = adds[x] + xf[pl.ds((side * 5 + i) * rows_y, rows_y), :]
-                    scale = weight * rx[0, side, len(raw_x[up]) + place(buo_x[up], x)]
-                    new = rx[step, side, len(raw_x[up]) + 2 + i] + scale * add
+                    scale = weight * rx[0, side, len(raw_x[up]) + len(flow_x[up]) + place(buo_x[up], x)]
+                    new = rx[step, side, len(raw_x[up]) + i] + scale * add
                     at = x - rows_x if up else x + rows_x
                     vb[pl.ds(vb_row(step, k, at), rows_y), :] = new
+
+    def buo_halo_y(up, c, y):
+        i = len(raw_y[up]) + len(flow_y[up]) + place(buo_y[up], y)
+        return ry[0, int(up), c, pl.ds(i * 8, 8), :]
 
     def finish_y(step, c):
         for up in (True, False):
@@ -423,14 +430,19 @@
                 adds = dict(spread(kind, not up, rows_y, lambda i: sy_pack(step, comp, c, mine[i])))
                 for y in edge(FLOW_Y[k], up, rows_y):
                     i = place(flow_y[up], (k, y))
-                    add = adds[y]
-                    for end, at_end in ((1, 0), (0, chunks - 1)):
-                        if c == at_end:
-                            add = add + yf[pl.ds(((side * 5 + i) * 2 + end) * 8, 8), :]
-                    scale = weight * ry[0, side, c, pl.ds((len(raw_y[up]) + place(buo_y[up], y)) * 8, 8), :]
-                    new = got(len(raw_y[up]) + 2 + i) + scale * add
+                    scale = weight * buo_halo_y(up, c, y)
+                    new = got(len(raw_y[up]) + i) + scale * adds[y]
                     at = y - rows_y if up else y + rows_y
                     vb[vb_pack(step, k, c, at), :] = new
+
+    def finish_corners_y(step):
+        for up in (True, False):
+            for i, (k, y) in enumerate(flow_y[up]):
+                at = y - rows_y if up else y + rows_y
+                for end, c in ((1, 0), (0, chunks - 1)):
+                    add = yf[pl.ds(((int(up) * 5 + i) * 2 + end) * 8, 8), :]
+                    where = vb_pack(step, k, c, at)
+                    vb[where, :] = vb[where, :] + weight * buo_halo_y(up, c, y) * add
 
     def stress_layer(step, x):
         last = step == STEPS - 1
@@ -487,31 +499,25 @@
         return carry
 
     lax.fori_loop(0, rows_x, fill_y, 0, unroll=8)
+    for copy in loads[first:second]:
+        copy.wait()
+    ends = [0] + ([chunks - 1] if chunks > 1 else [])
+    middle = list(range(1, chunks - 1))
     for up in (True, False):
         pack_x_raw(0, up)
     pack_corners(0, (True, False))
-    for c in range(chunks):
+    for c in ends + middle:
         pack_y_raw(0, c)
+        for i in range(CH):
+            flow_layer(0, c * CH + i)
+        pack_y_flow(0, c)
+    for up in (True, False):
+        pack_x_flow(0, up)
     heard = sum(there.astype(jnp.int32) for there, _ in sides)
     pl.semaphore_wait(barrier, heard)
-    for up in (True, False):
-        send_x(0, up, (0,))
     send_corners(0, (True, False))
-    send_y(0, range(chunks), (0,))
-    for copy in loads[first:second]:
-        copy.wait()
-    order = [0] + ([chunks - 1] if chunks > 1 else []) + list(range(1, chunks - 1))
-    for c in order:
-        for i in range(CH):
-            flow_layer(0, c * CH + i)
-        if c == 0:
-            pack_x_flow(0, False)
-            send_x(0, False, (1,))
-        if c == chunks - 1:
-            pack_x_flow(0, True)
-            send_x(0, True, (1,))
-        pack_y_flow(0, c)
-        send_y(0, (c,), (1,))
+    send_x(0, 0)
+    send_y(0, ends + middle, (0,))
 
     cell = cell_ref[...]
     bits = depth.bit_length() - 1
@@ -535,6 +541,7 @@
         )
         inj[comp] = value.reshape(rows_x, rows_y, depth)
 
+    send_x(0, 1)
     for copy in loads[second:third]:
         copy.wait()
     frictions, cohesions = [], []
@@ -560,65 +567,72 @@
     for copy in loads[third:]:
         copy.wait()
 
+    rim = [x for x in range(rows_x) if x < 4 or x >= rows_x - 4]
+    near = [x for x in range(rows_x) if x not in rim and (x < CH + 2 or x >= rows_x - CH - 2)]
+    inner = [x for x in range(rows_x) if x not in rim and x not in near]
     for step in range(STEPS):
+        nxt = step + 1
+        last = nxt == STEPS
+        wait_y(step, ends)
+        for c in ends:
+            finish_y(step, c)
         wait_corners(step)
         take_corners(step)
+        finish_corners_y(step)
         wait_x(step)
         finish_x(step)
-        wait_y(step)
-        for c in range(chunks):
+        for x in rim:
+            stress_layer(step, x)
+        flowed = set()
+        if not last:
+            pack_corners(nxt, (True, False))
+            send_corners(nxt, (True, False))
+            for x in (0, 1, rows_x - 2, rows_x - 1):
+                flow_layer(nxt, x)
+                flowed.add(x)
+            for up in (True, False):
+                pack_x_raw(nxt, up)
+                pack_x_flow(nxt, up)
+            send_x(nxt, 0)
+        wait_y(step, middle)
+        for c in middle:
             finish_y(step, c)
-        last = step == STEPS - 1
-        done = 0
-        stressed = set()
-        flowed = set()
-        sent = set()
-        for c in order:
-            for i in range(CH):
-                stress_layer(step, c * CH + i)
-            if last:
-                continue
-            nxt = step + 1
-            stressed.update(range(c * CH, (c + 1) * CH))
-            pack_y_raw(nxt, c)
-            send_y(nxt, (c,), (0,))
-            if c == 0:
-                pack_corners(nxt, (False,))
-                send_corners(nxt, (False,))
-                pack_x_raw(nxt, False)
-            if c == chunks - 1:
-                pack_corners(nxt, (True,))
-                send_corners(nxt, (True,))
-                pack_x_raw(nxt, True)
-            for x in range(rows_x):
-                near = range(max(x - 2, 0), min(x + 3, rows_x))
-                if x not in flowed and all(n in stressed for n in near):
+        for x in near:
+            stress_layer(step, x)
+        if not last:
+            for c in ends:
+                pack_y_raw(nxt, c)
+            send_y(nxt, ends, (0,))
+            for c in ends:
+                for x in range(c * CH, (c + 1) * CH):
+                    if x not in flowed:
+                        flow_layer(nxt, x)
+                pack_y_flow(nxt, c)
+            send_y(nxt, ends, (1,))
+            send_x(nxt, 1)
+        for x in inner:
+            stress_layer(step, x)
+        if not last:
+            for c in middle:
+                pack_y_raw(nxt, c)
+            send_y(nxt, middle, (0,))
+            for c in middle:
+                for x in range(c * CH, (c + 1) * CH):
                     flow_layer(nxt, x)
-                    flowed.add(x)
-            if c == 0:
-                pack_x_flow(nxt, False)
-                send_x(nxt, False, (0, 1))
-            if c == chunks - 1:
-                pack_x_flow(nxt, True)
-                send_x(nxt, True, (0, 1))
-            for other in order:
-                if other not in sent and all(x in flowed for x in range(other * CH, (other + 1) * CH)):
-                    pack_y_flow(nxt, other)
-                    send_y(nxt, (other,), (1,))
-                    sent.add(other)
+                pack_y_flow(nxt, c)
+                send_y(nxt, (c,), (1,))
 
     for step in range(STEPS):
         for up in (True, False):
 
             @pl.when(to_x(up)[0])
             def _():
-                for part in (0, 1):
-                    x_copy(step, up, part).wait_send()
+                x_copy(step, up).wait_send()
 
             @pl.when(to_y(up)[0])
             def _():
                 for c in range(chunks):
-                    for part in (0, 1):
+                    for part in y_parts(step):
                         y_copy(step, up, c, part).wait_send()
 
         for d, (cx, cy) in enumerate(CORNERS):
@@ -630,7 +644,7 @@
 
 def on_device(nx, ny, velocity, stress, lame_first, modulus, buoyancy, zone, eligible, cohesion, friction, source_cell, source_moment):
     rows_x, rows_y, depth = zone.shape
-    assert rows_y == 8 and rows_x % CH == 0
+    assert rows_y == 8 and rows_x % CH == 0 and rows_x >= 3 * CH
     chunks = rows_x // CH
     f32 = jnp.float32
     grid = (rows_x, rows_y, depth)
@@ -668,8 +682,8 @@
             pltpu.VMEM((2 * 5 * rows_y, depth), f32),
             pltpu.VMEM((2 * 5 * 2 * 8, depth), f32),
             dma((12,)),
-            dma((STEPS, 2, 2)),
-            dma((STEPS, 2, 2)),
+            dma((STEPS, 2)),
+            dma((STEPS, 2)),
             dma((STEPS, 2, chunks, 2)),
             dma((STEPS, 2, chunks, 2)),
             dma((STEPS, 4)),

time: 17.9 us -> 17.5 us (0.978)
  Pallas kernels: 15.4 us -> 15 us
    pallas_call x1, Pallas kernels: 15.4 us -> 15 us  [on_device(): pl.pallas_call(functools.partial(kernel, nx, ny), out_shape=(pltpu.VMEM((...]
where the time goes in v2:
time: 17.5 us; the launch traced here: 17.3 us
  Pallas kernels  15 us (86%)
  local copies, waits for them, and re-layouts  1.63 us (9%)
  between operations  0.64 us (4%)
    pallas_call x1, Pallas kernels, on_device(): pl.pallas_call(functools.partial(kernel, nx, ny), out_shape=(pltpu.VMEM((...  15 us
    unnamed x2, local copies, waits for them, and re-layouts  1.63 us

profile of v2, /device:TPU:1, one launch (start us, length us, event | category | flops | bytes accessed | tf_op | source)
XLA Modules:
  0.0 17.3 jit_solution(5186411544124588795)
XLA Ops:
  0.6 15.0 %shard_map.122 = (f32[3,32,8,128]{3,2,1,0:T(8,128)S(1)}, f32[6,32,8,128]{3,2,1,0:T(8,128)S(1)}) custom-call(f32[768,128]{1,0:T(8,128)} %bitcast.5, f32[1536,128]{1,0:T(8,128)} %bitcast.4, f32[32,8,128]{2,1,0:T(8,128)} %lam_hbm.1, f32[32,8,128]{2,1,0:T(8,128)} %mod_hbm.1, f32[256,128]{1,0:T(8,128)} %bitcast.6, s32[32,8,128]{2,1,0:T(8,128)} %zone_hbm.1, ...), custom_call_target="tpu_custom_call" | custom-call | tf_op jit(solution)/shard_map/pallas_call | solution.py:656
  15.7 0.7 %copy.15 = f32[3,32,8,128]{3,2,1,0:T(8,128)} copy(f32[3,32,8,128]{3,2,1,0:T(8,128)S(1)} %get-tuple-element.2) | data formatting | bytes 786432
  16.4 0.9 %copy.16 = f32[6,32,8,128]{3,2,1,0:T(8,128)} copy(f32[6,32,8,128]{3,2,1,0:T(8,128)S(1)} %get-tuple-element.3) | data formatting | bytes 1572864

commit v3 on v2

--- a/solution.py
+++ b/solution.py
@@ -56,7 +56,119 @@
     return list(dict.fromkeys(found))
 
 
-CORNERS = [(True, True), (True, False), (False, True), (False, False)]
+CORNERS = [(False, True), (False, False), (True, True), (True, False)]
+
+
+class Fields:
+    def __init__(self, sx, sy, zb, vb, lam, mod, inj, cc, cf):
+        self.sx, self.sy, self.zb, self.vb = sx, sy, zb, vb
+        self.lam, self.mod, self.inj, self.cc, self.cf = lam, mod, inj, cc, cf
+        self.rows_x, self.rows_y, self.depth = lam.shape
+        lane = lax.broadcasted_iota(jnp.int32, (self.rows_y, self.depth), 1)
+        self.keep = {1: lane < self.depth - 1, 2: lane < self.depth - 2, -1: lane >= 1, -2: lane >= 2}
+
+    def sx_row(self, comp, x):
+        return (SLOT_X[comp] * (self.rows_x + 4) + x + 2) * self.rows_y
+
+    def sy_row(self, comp, x):
+        return SLOT_Y[comp] * R * (self.rows_x + 1) + R * (x + 1)
+
+    def vb_row(self, slot, x):
+        return (slot * (self.rows_x + 5) + x + 3) * R
+
+    def sx_tile(self, step, comp, x):
+        return self.sx[step][pl.ds(self.sx_row(comp, x), self.rows_y), :]
+
+    def own_sy(self, step, comp, x):
+        return self.sy[step][pl.ds(self.sy_row(comp, x), self.rows_y), :]
+
+    def own_zb(self, step, x):
+        return self.zb[step][pl.ds(x * self.rows_y, self.rows_y), :]
+
+    def own_v(self, step, slot, x):
+        return self.vb[step][pl.ds(self.vb_row(slot, x), self.rows_y), :]
+
+    def along_z(self, value, offset):
+        if offset == 0:
+            return value
+        return jnp.where(self.keep[offset], pltpu.roll(value, (-offset) % self.depth, 1), 0.0)
+
+    def derivative(self, get, forward):
+        a, b, c, d = (get(1), get(0), get(2), get(-1)) if forward else (get(0), get(-1), get(1), get(-2))
+        return 27.0 * (a - b) - (c - d)
+
+    def s_dx(self, step, comp, x, forward):
+        return self.derivative(lambda o: self.sx_tile(step, comp, x + o), forward)
+
+    def s_dy(self, step, comp, x, forward):
+        row = self.sy_row(comp, x)
+        return self.derivative(lambda o: self.sy[step][pl.ds(row + o, self.rows_y), :], forward)
+
+    def v_dx(self, step, slot, x, forward):
+        return self.derivative(lambda o: self.own_v(step, slot, x + o), forward)
+
+    def v_dy(self, step, slot, x, forward):
+        row = self.vb_row(slot, x)
+        return self.derivative(lambda o: self.vb[step][pl.ds(row + o, self.rows_y), :], forward)
+
+    def dz(self, value, forward):
+        return self.derivative(lambda o: self.along_z(value, o), forward)
+
+    def forces(self, step, x):
+        xz, yz, zz = self.sx_tile(step, 4, x), self.own_sy(step, 5, x), self.own_zb(step, x)
+        return (
+            self.s_dx(step, 0, x, True) + self.s_dy(step, 3, x, False) + self.dz(xz, False),
+            self.s_dx(step, 3, x, False) + self.s_dy(step, 1, x, True) + self.dz(yz, False),
+            self.s_dx(step, 4, x, False) + self.s_dy(step, 5, x, False) + self.dz(zz, True),
+        )
+
+    def stress(self, step, x):
+        vx, vy, vz = (self.own_v(step, slot, x) for slot in range(3))
+        ex = self.v_dx(step, 0, x, False)
+        ey = self.v_dy(step, 1, x, False)
+        ez = self.dz(vz, False)
+        xy = self.v_dy(step, 0, x, True) + self.v_dx(step, 1, x, True)
+        xz = self.dz(vx, True) + self.v_dx(step, 2, x, True)
+        yz = self.dz(vy, True) + self.v_dy(step, 2, x, True)
+        weight = time_step / 24.0
+        inj = self.inj
+        m = weight * self.mod[x]
+        grow = weight * self.lam[x] * (ex + ey + ez)
+        m2 = m + m
+        s0, s3, s4 = (self.sx_tile(step, comp, x) for comp in (0, 3, 4))
+        s1, s5 = self.own_sy(step, 1, x), self.own_sy(step, 5, x)
+        s2 = self.own_zb(step, x)
+        s0 = s0 + (grow + m2 * ex) + inj[0, x]
+        s1 = s1 + (grow + m2 * ey) + inj[1, x]
+        s2 = s2 + (grow + m2 * ez) + inj[2, x]
+        s3 = s3 + m * xy + inj[3, x]
+        s4 = s4 + m * xz + inj[4, x]
+        s5 = s5 + m * yz + inj[5, x]
+        pressure = (s0 + s1 + s2) * (1.0 / 3.0)
+        d0, d1, d2 = s0 - pressure, s1 - pressure, s2 - pressure
+        second = 0.5 * (d0 * d0 + d1 * d1 + d2 * d2) + (s3 * s3 + s4 * s4 + s5 * s5)
+        strength = jnp.maximum(self.cc[x] - pressure * self.cf[x], 0.0)
+        factor = jnp.minimum(1.0, strength * lax.rsqrt(jnp.maximum(second, shear_floor * shear_floor)))
+        s0, s1, s2 = pressure + factor * d0, pressure + factor * d1, pressure + factor * d2
+        return s0, s1, s2, factor * s3, factor * s4, factor * s5
+
+
+def finish_kernel(sx, sy, zb, vb, lam, mod, inj, cc, cf, vout_hbm, sout_hbm, vout, sout, sem):
+    at = Fields((None, sx), (None, sy), (None, zb), (None, vb), lam, mod, inj, cc, cf)
+    copies = []
+    for c in range(at.rows_x // CH):
+        for x in range(c * CH, (c + 1) * CH):
+            for slot in range(3):
+                vout[slot, x] = at.own_v(STEPS - 1, slot, x)
+            for comp, value in enumerate(at.stress(STEPS - 1, x)):
+                sout[comp, x] = value
+        for i, (src, dst) in enumerate(((vout, vout_hbm), (sout, sout_hbm))):
+            layers = pl.ds(c * CH, CH)
+            copy = pltpu.make_async_copy(src.at[:, layers], dst.at[:, layers], sem.at[c, i])
+            copy.start()
+            copies.append(copy)
+    for copy in copies:
+        copy.wait()
 
 
 def kernel(
@@ -64,15 +176,18 @@
     ny,
     vel_hbm, str_hbm, lam_hbm, mod_hbm, buo_hbm, zone_hbm, elig_hbm,
     coh_ref, fri_ref, cell_ref, moment_ref,
-    vout_ref, sout_ref,
-    stage, vel, lam, mod, buo, zone, elig, inj, cc, cf,
-    sx, sy, zb, vb, xs, rx, ys, ry, ds, rd, xf, yf,
+    sx1, sy1, zb1, vb1, lam, mod, inj, cc, cf,
+    sx0, sy0, zb0, vb0, stage, vel, buo, zone, elig,
+    xs, rx, ys, ry, ds, rd, xf, yf,
     load_sem, xsend, xrecv, ysend, yrecv, dsend, drecv,
 ):
     rows_x = lam.shape[0]
     rows_y = lam.shape[1]
     depth = lam.shape[2]
     chunks = rows_x // CH
+    sx, sy, zb, vb = (sx0, sx1), (sy0, sy1), (zb0, zb1), (vb0, vb1)
+    at = Fields(sx, sy, zb, vb, lam, mod, inj, cc, cf)
+    sx_row, sy_row, vb_row, sx_tile = at.sx_row, at.sy_row, at.vb_row, at.sx_tile
     ix = lax.axis_index("gx")
     iy = lax.axis_index("gy")
     x_lo, x_hi, y_lo, y_hi = ix > 0, ix < nx - 1, iy > 0, iy < ny - 1
@@ -110,24 +225,15 @@
         copy.start()
         loads.append(copy)
 
-    def sx_row(step, comp, x):
-        return ((step * 3 + SLOT_X[comp]) * (rows_x + 4) + x + 2) * rows_y
-
-    def sy_row(step, comp, x):
-        return (step * 3 + SLOT_Y[comp]) * R * (rows_x + 1) + R * (x + 1)
-
-    def vb_row(step, slot, x):
-        return ((step * 3 + slot) * (rows_x + 5) + x + 3) * R
-
     plane = rows_x * rows_y
-    load(str_hbm.at[pl.ds(3 * plane, plane)], sx.at[pl.ds(sx_row(0, 3, 0), plane)])
+    load(str_hbm.at[pl.ds(3 * plane, plane)], sx0.at[pl.ds(sx_row(3, 0), plane)])
     load(str_hbm.at[pl.ds(1 * plane, plane)], stage.at[0])
     load(str_hbm.at[pl.ds(5 * plane, plane)], stage.at[1])
     load(buo_hbm, buo)
-    load(str_hbm.at[pl.ds(0 * plane, plane)], sx.at[pl.ds(sx_row(0, 0, 0), plane)])
-    load(str_hbm.at[pl.ds(4 * plane, plane)], sx.at[pl.ds(sx_row(0, 4, 0), plane)])
+    load(str_hbm.at[pl.ds(0 * plane, plane)], sx0.at[pl.ds(sx_row(0, 0), plane)])
+    load(str_hbm.at[pl.ds(4 * plane, plane)], sx0.at[pl.ds(sx_row(4, 0), plane)])
     first = len(loads)
-    load(str_hbm.at[pl.ds(2 * plane, plane)], zb.at[pl.ds(0, plane)])
+    load(str_hbm.at[pl.ds(2 * plane, plane)], zb0)
     load(vel_hbm, vel)
     second = len(loads)
     load(zone_hbm, zone)
@@ -141,16 +247,17 @@
     for step in range(STEPS):
         for comp in SLOT_X:
             for layer in (-2, -1, rows_x, rows_x + 1):
-                sx[pl.ds(sx_row(step, comp, layer), rows_y), :] = tile
+                sx[step][pl.ds(sx_row(comp, layer), rows_y), :] = tile
     for ref in (xf, yf):
         for i in range(ref.shape[0] // rows_y):
             ref[pl.ds(i * rows_y, rows_y), :] = tile
 
     def clear(i, carry):
-        sy[pl.ds(pl.multiple_of(i * R + rows_y, 8), R - rows_y), :] = jnp.zeros((R - rows_y, depth), jnp.float32)
+        for ref in sy:
+            ref[pl.ds(pl.multiple_of(i * R + rows_y, 8), R - rows_y), :] = jnp.zeros((R - rows_y, depth), jnp.float32)
         return carry
 
-    lax.fori_loop(0, sy.shape[0] // R, clear, 0, unroll=8)
+    lax.fori_loop(0, sy0.shape[0] // R, clear, 0, unroll=4)
 
     for up in (True, False):
 
@@ -215,14 +322,11 @@
             device_id_type=MESH,
         )
 
-    def sx_tile(step, comp, x):
-        return sx[pl.ds(sx_row(step, comp, x), rows_y), :]
-
     def sy_pack(step, comp, c, row):
-        return sy[pl.ds(sy_row(step, comp, c * CH) + row, CH, stride=R), :]
-
-    def vb_pack(step, slot, c, row):
-        return pl.ds(vb_row(step, slot, c * CH) + row, CH, stride=R)
+        return sy[step][pl.ds(sy_row(comp, c * CH) + row, CH, stride=R), :]
+
+    def vb_pack(slot, c, row):
+        return pl.ds(vb_row(slot, c * CH) + row, CH, stride=R)
 
     def pack_x_raw(step, up):
         for i, (comp, x) in enumerate(raw_x[up]):
@@ -242,29 +346,28 @@
 
     def pack_x_flow(step, up):
         for i, (slot, x) in enumerate(flow_x[up]):
-            xs[step, int(up), len(raw_x[up]) + i] = vb[pl.ds(vb_row(step, slot, x), rows_y), :]
+            xs[step, int(up), len(raw_x[up]) + i] = vb[step][pl.ds(vb_row(slot, x), rows_y), :]
 
     def pack_y_flow(step, c):
         for up in (True, False):
             for i, (slot, row) in enumerate(flow_y[up]):
-                ys[step, int(up), c, pl.ds((len(raw_y[up]) + i) * 8, 8), :] = vb[vb_pack(step, slot, c, row), :]
+                ys[step, int(up), c, pl.ds((len(raw_y[up]) + i) * 8, 8), :] = vb[step][vb_pack(slot, c, row), :]
 
     def pack_corners(step, cxs):
         for d, (cx, cy) in enumerate(CORNERS):
             if cx in cxs:
                 for i, (comp, x, y) in enumerate(corner[(cx, cy)]):
                     if comp in SLOT_X:
-                        value = sx[pl.ds(sx_row(step, comp, x) + y, 1), :]
+                        value = sx[step][pl.ds(sx_row(comp, x) + y, 1), :]
                     else:
-                        value = sy[pl.ds(sy_row(step, comp, x) + y, 1), :]
+                        value = sy[step][pl.ds(sy_row(comp, x) + y, 1), :]
                     ds[step, d, pl.ds(i, 1), :] = value
 
-    def send_x(step, core):
-        mine = iy % 2 == core
-        odd = ix % 2 == 1
-        for up, when in ((True, odd), (False, True), (True, jnp.logical_not(odd))):
-
-            @pl.when(jnp.logical_and(jnp.logical_and(to_x(up)[0], mine), when))
+    def send_x(step, cores):
+        mine = iy % 2 == cores[0]
+        for up in (False, True):
+
+            @pl.when(to_x(up)[0] if len(cores) == 2 else jnp.logical_and(to_x(up)[0], mine))
             def _():
                 x_copy(step, up).start()
 
@@ -285,63 +388,24 @@
                 def _():
                     d_copy(step, d).start()
 
-    lane = lax.broadcasted_iota(jnp.int32, (rows_y, depth), 1)
-    keep = {
-        1: lane < depth - 1,
-        2: lane < depth - 2,
-        -1: lane >= 1,
-        -2: lane >= 2,
-    }
-
-    def along_z(value, offset):
-        if offset == 0:
-            return value
-        return jnp.where(keep[offset], pltpu.roll(value, (-offset) % depth, 1), 0.0)
-
-    def derivative(get, forward):
-        a, b, c, d = (get(1), get(0), get(2), get(-1)) if forward else (get(0), get(-1), get(1), get(-2))
-        return 27.0 * (a - b) - (c - d)
-
-    def s_dx(step, comp, x, forward):
-        return derivative(lambda o: sx_tile(step, comp, x + o), forward)
-
-    def s_dy(step, comp, x, forward):
-        return derivative(lambda o: sy[pl.ds(sy_row(step, comp, x) + o, rows_y), :], forward)
-
-    def v_dx(step, slot, x, forward):
-        return derivative(lambda o: vb[pl.ds(vb_row(step, slot, x + o), rows_y), :], forward)
-
-    def v_dy(step, slot, x, forward):
-        return derivative(lambda o: vb[pl.ds(vb_row(step, slot, x) + o, rows_y), :], forward)
-
-    def dz(value, forward):
-        return derivative(lambda o: along_z(value, o), forward)
-
-    def own_sy(step, comp, x):
-        return sy[pl.ds(sy_row(step, comp, x), rows_y), :]
-
-    def own_zb(step, x):
-        return zb[pl.ds((step * rows_x + x) * rows_y, rows_y), :]
-
-    def own_v(step, slot, x):
-        return vb[pl.ds(vb_row(step, slot, x), rows_y), :]
+    weight = time_step / 24.0
+
+    def flow_layer(step, x):
+        scale = weight * of_cell(buo, x)
+        for slot, force in enumerate(at.forces(step, x)):
+            old = vel[pl.ds((slot * rows_x + x) * rows_y, rows_y), :] if step == 0 else at.own_v(step - 1, slot, x)
+            vb[step][pl.ds(vb_row(slot, x), rows_y), :] = old + scale * force
+
+    def stress_layer(step, x):
+        s = at.stress(step, x)
+        for comp in SLOT_X:
+            sx[step + 1][pl.ds(sx_row(comp, x), rows_y), :] = s[comp]
+        for comp in SLOT_Y:
+            sy[step + 1][pl.ds(sy_row(comp, x), rows_y), :] = s[comp]
+        zb[step + 1][pl.ds(x * rows_y, rows_y), :] = s[2]
 
     def of_cell(ref, x):
         return ref[pl.ds(x * rows_y, rows_y), :]
-
-    weight = time_step / 24.0
-
-    def flow_layer(step, x):
-        scale = weight * of_cell(buo, x)
-        xz = sx_tile(step, 4, x)
-        yz = own_sy(step, 5, x)
-        zz = own_zb(step, x)
-        force_x = s_dx(step, 0, x, True) + s_dy(step, 3, x, False) + dz(xz, False)
-        force_y = s_dx(step, 3, x, False) + s_dy(step, 1, x, True) + dz(yz, False)
-        force_z = s_dx(step, 4, x, False) + s_dy(step, 5, x, False) + dz(zz, True)
-        for slot, force in enumerate((force_x, force_y, force_z)):
-            old = vel[pl.ds((slot * rows_x + x) * rows_y, rows_y), :] if step == 0 else own_v(step - 1, slot, x)
-            vb[pl.ds(vb_row(step, slot, x), rows_y), :] = old + scale * force
 
     def wait_x(step):
         for up in (True, False):
@@ -395,8 +459,8 @@
             for k, (comp, kind) in enumerate(FORCE_X):
                 places = [place(raw_x[up], (comp, x)) for x in edge(kind, up, rows_x)]
                 for x, value in spread(kind, up, rows_x, lambda i: rx[step, side, places[i]]):
-                    where = pl.ds(vb_row(step, k, x), rows_y)
-                    vb[where, :] = vb[where, :] + weight * of_cell(buo, x) * value
+                    where = pl.ds(vb_row(k, x), rows_y)
+                    vb[step][where, :] = vb[step][where, :] + weight * of_cell(buo, x) * value
             for k, (comp, kind) in enumerate(FORCE_X):
                 mine = edge(kind, not up, rows_x)
                 adds = dict(spread(kind, not up, rows_x, lambda i: sx_tile(step, comp, mine[i])))
@@ -405,8 +469,8 @@
                     add = adds[x] + xf[pl.ds((side * 5 + i) * rows_y, rows_y), :]
                     scale = weight * rx[0, side, len(raw_x[up]) + len(flow_x[up]) + place(buo_x[up], x)]
                     new = rx[step, side, len(raw_x[up]) + i] + scale * add
-                    at = x - rows_x if up else x + rows_x
-                    vb[pl.ds(vb_row(step, k, at), rows_y), :] = new
+                    halo = x - rows_x if up else x + rows_x
+                    vb[step][pl.ds(vb_row(k, halo), rows_y), :] = new
 
     def buo_halo_y(up, c, y):
         i = len(raw_y[up]) + len(flow_y[up]) + place(buo_y[up], y)
@@ -422,9 +486,9 @@
             for k, (comp, kind) in enumerate(FORCE_Y):
                 places = [place(raw_y[up], (comp, y)) for y in edge(kind, up, rows_y)]
                 for y, value in spread(kind, up, rows_y, lambda i: got(places[i])):
-                    where = vb_pack(step, k, c, y)
+                    where = vb_pack(k, c, y)
                     scale = weight * buo[pl.ds(c * CH * rows_y + y, CH, stride=rows_y), :]
-                    vb[where, :] = vb[where, :] + scale * value
+                    vb[step][where, :] = vb[step][where, :] + scale * value
             for k, (comp, kind) in enumerate(FORCE_Y):
                 mine = edge(kind, not up, rows_y)
                 adds = dict(spread(kind, not up, rows_y, lambda i: sy_pack(step, comp, c, mine[i])))
@@ -432,70 +496,29 @@
                     i = place(flow_y[up], (k, y))
                     scale = weight * buo_halo_y(up, c, y)
                     new = got(len(raw_y[up]) + i) + scale * adds[y]
-                    at = y - rows_y if up else y + rows_y
-                    vb[vb_pack(step, k, c, at), :] = new
+                    halo = y - rows_y if up else y + rows_y
+                    vb[step][vb_pack(k, c, halo), :] = new
 
     def finish_corners_y(step):
         for up in (True, False):
             for i, (k, y) in enumerate(flow_y[up]):
-                at = y - rows_y if up else y + rows_y
+                halo = y - rows_y if up else y + rows_y
                 for end, c in ((1, 0), (0, chunks - 1)):
                     add = yf[pl.ds(((int(up) * 5 + i) * 2 + end) * 8, 8), :]
-                    where = vb_pack(step, k, c, at)
-                    vb[where, :] = vb[where, :] + weight * buo_halo_y(up, c, y) * add
-
-    def stress_layer(step, x):
-        last = step == STEPS - 1
-        vx, vy, vz = (own_v(step, slot, x) for slot in range(3))
-        if last:
-            for slot, value in enumerate((vx, vy, vz)):
-                vout_ref[slot, x] = value
-        ex = v_dx(step, 0, x, False)
-        ey = v_dy(step, 1, x, False)
-        ez = dz(vz, False)
-        xy = v_dy(step, 0, x, True) + v_dx(step, 1, x, True)
-        xz = dz(vx, True) + v_dx(step, 2, x, True)
-        yz = dz(vy, True) + v_dy(step, 2, x, True)
-        m = weight * mod[x]
-        grow = weight * lam[x] * (ex + ey + ez)
-        m2 = m + m
-        s0, s3, s4 = (sx_tile(step, comp, x) for comp in (0, 3, 4))
-        s1, s5 = own_sy(step, 1, x), own_sy(step, 5, x)
-        s2 = own_zb(step, x)
-        s0 = s0 + (grow + m2 * ex) + inj[0, x]
-        s1 = s1 + (grow + m2 * ey) + inj[1, x]
-        s2 = s2 + (grow + m2 * ez) + inj[2, x]
-        s3 = s3 + m * xy + inj[3, x]
-        s4 = s4 + m * xz + inj[4, x]
-        s5 = s5 + m * yz + inj[5, x]
-        pressure = (s0 + s1 + s2) * (1.0 / 3.0)
-        d0, d1, d2 = s0 - pressure, s1 - pressure, s2 - pressure
-        second = 0.5 * (d0 * d0 + d1 * d1 + d2 * d2) + (s3 * s3 + s4 * s4 + s5 * s5)
-        strength = jnp.maximum(cc[x] - pressure * cf[x], 0.0)
-        factor = jnp.minimum(1.0, strength * lax.rsqrt(jnp.maximum(second, shear_floor * shear_floor)))
-        s0, s1, s2 = pressure + factor * d0, pressure + factor * d1, pressure + factor * d2
-        s3, s4, s5 = factor * s3, factor * s4, factor * s5
-        if last:
-            for comp, value in enumerate((s0, s1, s2, s3, s4, s5)):
-                sout_ref[comp, x] = value
-            return
-        for comp, value in ((0, s0), (3, s3), (4, s4)):
-            sx[pl.ds(sx_row(step + 1, comp, x), rows_y), :] = value
-        for comp, value in ((3, s3), (1, s1), (5, s5)):
-            sy[pl.ds(sy_row(step + 1, comp, x), rows_y), :] = value
-        zb[pl.ds(((step + 1) * rows_x + x) * rows_y, rows_y), :] = s2
+                    where = vb_pack(k, c, halo)
+                    vb[step][where, :] = vb[step][where, :] + weight * buo_halo_y(up, c, y) * add
 
     for copy in loads[:first]:
         copy.wait()
 
     def fill_y(i, carry):
-        at = pl.multiple_of(i * rows_y, 8)
+        first_row = pl.multiple_of(i * rows_y, 8)
         for comp, value in (
-            (3, sx[pl.ds(sx_row(0, 3, 0) + at, rows_y), :]),
-            (1, stage[0, pl.ds(at, rows_y), :]),
-            (5, stage[1, pl.ds(at, rows_y), :]),
+            (3, sx0[pl.ds(sx_row(3, 0) + first_row, rows_y), :]),
+            (1, stage[0, pl.ds(first_row, rows_y), :]),
+            (5, stage[1, pl.ds(first_row, rows_y), :]),
         ):
-            sy[pl.ds(pl.multiple_of(sy_row(0, comp, 0) + i * R, 8), rows_y), :] = value
+            sy0[pl.ds(pl.multiple_of(sy_row(comp, 0) + i * R, 8), rows_y), :] = value
         return carry
 
     lax.fori_loop(0, rows_x, fill_y, 0, unroll=8)
@@ -516,7 +539,7 @@
     heard = sum(there.astype(jnp.int32) for there, _ in sides)
     pl.semaphore_wait(barrier, heard)
     send_corners(0, (True, False))
-    send_x(0, 0)
+    send_x(0, (0,))
     send_y(0, ends + middle, (0,))
 
     cell = cell_ref[...]
@@ -541,7 +564,7 @@
         )
         inj[comp] = value.reshape(rows_x, rows_y, depth)
 
-    send_x(0, 1)
+    send_x(0, (1,))
     for copy in loads[second:third]:
         copy.wait()
     frictions, cohesions = [], []
@@ -581,8 +604,9 @@
         finish_corners_y(step)
         wait_x(step)
         finish_x(step)
-        for x in rim:
-            stress_layer(step, x)
+        if not last:
+            for x in rim:
+                stress_layer(step, x)
         flowed = set()
         if not last:
             pack_corners(nxt, (True, False))
@@ -593,13 +617,13 @@
             for up in (True, False):
                 pack_x_raw(nxt, up)
                 pack_x_flow(nxt, up)
-            send_x(nxt, 0)
+            send_x(nxt, (0,))
         wait_y(step, middle)
         for c in middle:
             finish_y(step, c)
-        for x in near:
-            stress_layer(step, x)
         if not last:
+            for x in near:
+                stress_layer(step, x)
             for c in ends:
                 pack_y_raw(nxt, c)
             send_y(nxt, ends, (0,))
@@ -609,10 +633,10 @@
                         flow_layer(nxt, x)
                 pack_y_flow(nxt, c)
             send_y(nxt, ends, (1,))
-            send_x(nxt, 1)
-        for x in inner:
-            stress_layer(step, x)
+            send_x(nxt, (1,))
         if not last:
+            for x in inner:
+                stress_layer(step, x)
             for c in middle:
                 pack_y_raw(nxt, c)
             send_y(nxt, middle, (0,))
@@ -653,26 +677,28 @@
     smem = pl.BlockSpec(memory_space=pltpu.SMEM)
     vmem = pl.BlockSpec(memory_space=pltpu.VMEM)
     dma = pltpu.SemaphoreType.DMA
-    return pl.pallas_call(
+    fields = [
+        pltpu.VMEM((3 * (rows_x + 4) * rows_y, depth), f32),
+        pltpu.VMEM((3 * R * (rows_x + 1) + R, depth), f32),
+        pltpu.VMEM((plane, depth), f32),
+        pltpu.VMEM((3 * (rows_x + 5) * R, depth), f32),
+        pltpu.VMEM(grid, f32),
+        pltpu.VMEM(grid, f32),
+        pltpu.VMEM((6,) + grid, f32),
+        pltpu.VMEM(grid, f32),
+        pltpu.VMEM(grid, f32),
+    ]
+    held = pl.pallas_call(
         functools.partial(kernel, nx, ny),
-        out_shape=(pltpu.VMEM((3,) + grid, f32), pltpu.VMEM((6,) + grid, f32)),
+        out_shape=fields,
         in_specs=[any_spec] * 7 + [smem, smem, vmem, vmem],
-        out_specs=(vmem, vmem),
-        scratch_shapes=[
+        out_specs=[vmem] * len(fields),
+        scratch_shapes=fields[:4] + [
             pltpu.VMEM((2, plane, depth), f32),
             pltpu.VMEM((3 * plane, depth), f32),
-            pltpu.VMEM(grid, f32),
-            pltpu.VMEM(grid, f32),
             pltpu.VMEM((plane, depth), f32),
             pltpu.VMEM(grid, jnp.int32),
             pltpu.VMEM(grid, jnp.int32),
-            pltpu.VMEM((6,) + grid, f32),
-            pltpu.VMEM(grid, f32),
-            pltpu.VMEM(grid, f32),
-            pltpu.VMEM((STEPS * 3 * (rows_x + 4) * rows_y, depth), f32),
-            pltpu.VMEM((STEPS * 3 * R * (rows_x + 1) + R, depth), f32),
-            pltpu.VMEM((STEPS * plane, depth), f32),
-            pltpu.VMEM((STEPS * 3 * (rows_x + 5) * R, depth), f32),
             pltpu.VMEM((STEPS, 2, 11, rows_y, depth), f32),
             pltpu.VMEM((STEPS, 2, 11, rows_y, depth), f32),
             pltpu.VMEM((STEPS, 2, chunks, 11 * 8, depth), f32),
@@ -689,12 +715,20 @@
             dma((STEPS, 4)),
             dma((STEPS, 4)),
         ],
-        compiler_params=pltpu.CompilerParams(collective_id=0, has_side_effects=True),
+        compiler_params=pltpu.CompilerParams(collective_id=0, has_side_effects=True, vmem_limit_bytes=63_000_000),
     )(
         velocity.reshape(3 * plane, depth), stress.reshape(6 * plane, depth), lame_first, modulus,
         buoyancy.reshape(plane, depth), zone, eligible,
         cohesion, friction, source_cell.reshape(1, -1), source_moment,
     )
+    return pl.pallas_call(
+        finish_kernel,
+        out_shape=(jax.ShapeDtypeStruct((3,) + grid, f32), jax.ShapeDtypeStruct((6,) + grid, f32)),
+        in_specs=[vmem] * len(fields),
+        out_specs=(any_spec, any_spec),
+        scratch_shapes=[pltpu.VMEM((3,) + grid, f32), pltpu.VMEM((6,) + grid, f32), dma((chunks, 2))],
+        compiler_params=pltpu.CompilerParams(vmem_limit_bytes=24 * 2**20),
+    )(*held)
 
 
 def solution(mesh):

time: 17.5 us -> 16.4 us (0.937)
  the two profiles are of different devices: /device:TPU:1 before, /device:TPU:21 now
where the time goes in v3:
time: 16.4 us; the launch traced here: 16.2 us
  Pallas kernels  15.6 us (95%)
  between operations  0.64 us (4%)
    pallas_call x1, Pallas kernels, on_device(): pl.pallas_call(functools.partial(kernel, nx, ny), out_shape=fields, in_sp...  14.2 us
    pallas_call x1, Pallas kernels, on_device(): pl.pallas_call(finish_kernel, out_shape=(jax.ShapeDtypeStruct((3,) + grid...  1.38 us

profile of v3, /device:TPU:21, one launch (start us, length us, event | category | flops | bytes accessed | tf_op | source)
XLA Modules:
  0.0 16.2 jit_solution(2863791931918691774)
XLA Ops:
  0.6 14.2 %shard_map.122 = (f32[864,128]{1,0:T(8,128)S(1)}, f32[1600,128]{1,0:T(8,128)S(1)}, f32[256,128]{1,0:T(8,128)S(1)}, f32[1776,128]{1,0:T(8,128)S(1)}, f32[32,8,128...) custom-call(f32[768,128]{1,0:T(8,128)} %bitcast.5, ...), custom_call_target="tpu_custom_call" | custom-call | tf_op jit(solution)/shard_map/pallas_call | solution.py:691
  14.8 1.4 %shard_map.123 = (f32[3,32,8,128]{3,2,1,0:T(8,128)}, f32[6,32,8,128]{3,2,1,0:T(8,128)}) custom-call(f32[864,128]{1,0:T(8,128)S(1)} %get-tuple-element.11.sx, f32[1600,128]{1,0:T(8,128)S(1)} %get-tuple-element.12.sy, f32[256,128]{1,0:T(8,128)S(1)} %get-tuple-element.13.zb, f32[1776,128]{1,0:T(8,128)S(1)} %get-tuple-element.14.vb, ...), custom_call_target="tpu_custom_call" | custom-call | tf_op jit(solution)/shard_map/pallas_call | solution.py:724

commit v4 on v3

--- a/solution.py
+++ b/solution.py
@@ -175,10 +175,10 @@
     nx,
     ny,
     vel_hbm, str_hbm, lam_hbm, mod_hbm, buo_hbm, zone_hbm, elig_hbm,
-    coh_ref, fri_ref, cell_ref, moment_ref,
+    coh_hbm, fri_hbm, cell_hbm, moment_hbm,
     sx1, sy1, zb1, vb1, lam, mod, inj, cc, cf,
     sx0, sy0, zb0, vb0, stage, vel, buo, zone, elig,
-    xs, rx, ys, ry, ds, rd, xf, yf,
+    xs, rx, ys, ry, ds, rd, xf, yf, coh_ref, fri_ref, cell_ref, moment_ref,
     load_sem, xsend, xrecv, ysend, yrecv, dsend, drecv,
 ):
     rows_x = lam.shape[0]
@@ -236,6 +236,11 @@
     load(str_hbm.at[pl.ds(2 * plane, plane)], zb0)
     load(vel_hbm, vel)
     second = len(loads)
+    load(cell_hbm, cell_ref)
+    load(moment_hbm, moment_ref)
+    sources = len(loads)
+    load(coh_hbm, coh_ref)
+    load(fri_hbm, fri_ref)
     load(zone_hbm, zone)
     load(elig_hbm, elig)
     third = len(loads)
@@ -529,19 +534,28 @@
     for up in (True, False):
         pack_x_raw(0, up)
     pack_corners(0, (True, False))
-    for c in ends + middle:
+
+    def flow_chunk(c):
         pack_y_raw(0, c)
         for i in range(CH):
             flow_layer(0, c * CH + i)
         pack_y_flow(0, c)
+
+    for c in ends:
+        flow_chunk(c)
     for up in (True, False):
         pack_x_flow(0, up)
     heard = sum(there.astype(jnp.int32) for there, _ in sides)
     pl.semaphore_wait(barrier, heard)
     send_corners(0, (True, False))
     send_x(0, (0,))
-    send_y(0, ends + middle, (0,))
-
+    send_y(0, ends, (0,))
+    for c in middle:
+        flow_chunk(c)
+        send_y(0, (c,), (0,))
+
+    for copy in loads[second:sources]:
+        copy.wait()
     cell = cell_ref[...]
     bits = depth.bit_length() - 1
     assert depth == 1 << bits
@@ -565,7 +579,7 @@
         inj[comp] = value.reshape(rows_x, rows_y, depth)
 
     send_x(0, (1,))
-    for copy in loads[second:third]:
+    for copy in loads[sources:third]:
         copy.wait()
     frictions, cohesions = [], []
     for which in range(coh_ref.shape[0]):
@@ -674,7 +688,6 @@
     grid = (rows_x, rows_y, depth)
     plane = rows_x * rows_y
     any_spec = pl.BlockSpec(memory_space=pltpu.HBM)
-    smem = pl.BlockSpec(memory_space=pltpu.SMEM)
     vmem = pl.BlockSpec(memory_space=pltpu.VMEM)
     dma = pltpu.SemaphoreType.DMA
     fields = [
@@ -691,7 +704,7 @@
     held = pl.pallas_call(
         functools.partial(kernel, nx, ny),
         out_shape=fields,
-        in_specs=[any_spec] * 7 + [smem, smem, vmem, vmem],
+        in_specs=[any_spec] * 11,
         out_specs=[vmem] * len(fields),
         scratch_shapes=fields[:4] + [
             pltpu.VMEM((2, plane, depth), f32),
@@ -707,7 +720,11 @@
             pltpu.VMEM((STEPS, 4, 16, depth), f32),
             pltpu.VMEM((2 * 5 * rows_y, depth), f32),
             pltpu.VMEM((2 * 5 * 2 * 8, depth), f32),
-            dma((12,)),
+            pltpu.SMEM(cohesion.shape, f32),
+            pltpu.SMEM(friction.shape, f32),
+            pltpu.VMEM((1,) + source_cell.shape, jnp.int32),
+            pltpu.VMEM(source_moment.shape, f32),
+            dma((16,)),
             dma((STEPS, 2)),
             dma((STEPS, 2)),
             dma((STEPS, 2, chunks, 2)),

time: 16.4 us -> 15.3 us (0.933)
  Pallas kernels: 15.6 us -> 14.5 us
    pallas_call x1, Pallas kernels: 14.2 us -> 13.1 us  [on_device(): pl.pallas_call(functools.partial(kernel, nx, ny), out_shape=fields, in_sp...]
where the time goes in v4:
time: 15.3 us; the launch traced here: 15.2 us
  Pallas kernels  14.5 us (95%)
  between operations  0.64 us (4%)
    pallas_call x1, Pallas kernels, on_device(): pl.pallas_call(functools.partial(kernel, nx, ny), out_shape=fields, in_sp...  13.1 us
    pallas_call x1, Pallas kernels, on_device(): pl.pallas_call(finish_kernel, out_shape=(jax.ShapeDtypeStruct((3,) + grid...  1.38 us

profile of v4, /device:TPU:21, one launch (start us, length us, event | category | flops | bytes accessed | tf_op | source)
XLA Modules:
  0.0 15.2 jit_solution(8427903063026771697)
XLA Ops:
  0.6 13.1 %shard_map.122 = (f32[864,128]{1,0:T(8,128)S(1)}, f32[1600,128]{1,0:T(8,128)S(1)}, f32[256,128]{1,0:T(8,128)S(1)}, f32[1776,128]{1,0:T(8,128)S(1)}, f32[32,8,128...) custom-call(f32[768,128]{1,0:T(8,128)} %bitcast.5, ...), custom_call_target="tpu_custom_call" | custom-call | tf_op jit(solution)/shard_map/pallas_call | solution.py:704
  13.8 1.4 %shard_map.123 = (f32[3,32,8,128]{3,2,1,0:T(8,128)}, f32[6,32,8,128]{3,2,1,0:T(8,128)}) custom-call(f32[864,128]{1,0:T(8,128)S(1)} %get-tuple-element.11.sx, f32[1600,128]{1,0:T(8,128)S(1)} %get-tuple-element.12.sy, f32[256,128]{1,0:T(8,128)S(1)} %get-tuple-element.13.zb, f32[1776,128]{1,0:T(8,128)S(1)} %get-tuple-element.14.vb, ...), custom_call_target="tpu_custom_call" | custom-call | tf_op jit(solution)/shard_map/pallas_call | solution.py:741

commit v5 on v4

--- a/solution.py
+++ b/solution.py
@@ -153,20 +153,32 @@
         return s0, s1, s2, factor * s3, factor * s4, factor * s5
 
 
-def finish_kernel(sx, sy, zb, vb, lam, mod, inj, cc, cf, vout_hbm, sout_hbm, vout, sout, sem):
+def rim_of(rows_x):
+    return [*range(4), *range(rows_x - 4, rows_x)]
+
+
+def finish_kernel(sx, sy, zb, vb, lam, mod, inj, cc, cf, edge_out, vout_hbm, sout_hbm, vout, sout, sem):
     at = Fields((None, sx), (None, sy), (None, zb), (None, vb), lam, mod, inj, cc, cf)
     copies = []
-    for c in range(at.rows_x // CH):
-        for x in range(c * CH, (c + 1) * CH):
+
+    def put(src, dst):
+        copy = pltpu.make_async_copy(src, dst, sem.at[len(copies)])
+        copy.start()
+        copies.append(copy)
+
+    for i, x in ((0, 0), (4, at.rows_x - 4)):
+        put(edge_out.at[:, pl.ds(i, 4)], sout_hbm.at[:, pl.ds(x, 4)])
+    for start in range(4, at.rows_x - 4, CH):
+        stop = min(start + CH, at.rows_x - 4)
+        low, high = (0 if start == 4 else start), (at.rows_x if stop == at.rows_x - 4 else stop)
+        for x in range(low, high):
             for slot in range(3):
                 vout[slot, x] = at.own_v(STEPS - 1, slot, x)
+        put(vout.at[:, pl.ds(low, high - low)], vout_hbm.at[:, pl.ds(low, high - low)])
+        for x in range(start, stop):
             for comp, value in enumerate(at.stress(STEPS - 1, x)):
                 sout[comp, x] = value
-        for i, (src, dst) in enumerate(((vout, vout_hbm), (sout, sout_hbm))):
-            layers = pl.ds(c * CH, CH)
-            copy = pltpu.make_async_copy(src.at[:, layers], dst.at[:, layers], sem.at[c, i])
-            copy.start()
-            copies.append(copy)
+        put(sout.at[:, pl.ds(start, stop - start)], sout_hbm.at[:, pl.ds(start, stop - start)])
     for copy in copies:
         copy.wait()
 
@@ -176,7 +188,7 @@
     ny,
     vel_hbm, str_hbm, lam_hbm, mod_hbm, buo_hbm, zone_hbm, elig_hbm,
     coh_hbm, fri_hbm, cell_hbm, moment_hbm,
-    sx1, sy1, zb1, vb1, lam, mod, inj, cc, cf,
+    sx1, sy1, zb1, vb1, lam, mod, inj, cc, cf, edge_out,
     sx0, sy0, zb0, vb0, stage, vel, buo, zone, elig,
     xs, rx, ys, ry, ds, rd, xf, yf, coh_ref, fri_ref, cell_ref, moment_ref,
     load_sem, xsend, xrecv, ysend, yrecv, dsend, drecv,
@@ -368,9 +380,9 @@
                         value = sy[step][pl.ds(sy_row(comp, x) + y, 1), :]
                     ds[step, d, pl.ds(i, 1), :] = value
 
-    def send_x(step, cores):
+    def send_x(step, cores, ways):
         mine = iy % 2 == cores[0]
-        for up in (False, True):
+        for up in ways:
 
             @pl.when(to_x(up)[0] if len(cores) == 2 else jnp.logical_and(to_x(up)[0], mine))
             def _():
@@ -548,7 +560,7 @@
     heard = sum(there.astype(jnp.int32) for there, _ in sides)
     pl.semaphore_wait(barrier, heard)
     send_corners(0, (True, False))
-    send_x(0, (0,))
+    send_x(0, (0,), (False, True))
     send_y(0, ends, (0,))
     for c in middle:
         flow_chunk(c)
@@ -578,7 +590,7 @@
         )
         inj[comp] = value.reshape(rows_x, rows_y, depth)
 
-    send_x(0, (1,))
+    send_x(0, (1,), (False, True))
     for copy in loads[sources:third]:
         copy.wait()
     frictions, cohesions = [], []
@@ -604,12 +616,34 @@
     for copy in loads[third:]:
         copy.wait()
 
-    rim = [x for x in range(rows_x) if x < 4 or x >= rows_x - 4]
-    near = [x for x in range(rows_x) if x not in rim and (x < CH + 2 or x >= rows_x - CH - 2)]
-    inner = [x for x in range(rows_x) if x not in rim and x not in near]
+    def finish_sends(step):
+        for up in (True, False):
+
+            @pl.when(to_x(up)[0])
+            def _():
+                x_copy(step, up).wait_send()
+
+            @pl.when(to_y(up)[0])
+            def _():
+                for c in range(chunks):
+                    for part in y_parts(step):
+                        y_copy(step, up, c, part).wait_send()
+
+        for d, (cx, cy) in enumerate(CORNERS):
+
+            @pl.when(to_corner(cx, cy)[0])
+            def _():
+                d_copy(step, d).wait_send()
+
+    def flow_rest(step, c, done):
+        for x in range(c * CH, (c + 1) * CH):
+            if x not in done:
+                flow_layer(step, x)
+        pack_y_flow(step, c)
+        send_y(step, (c,), (1,))
+
     for step in range(STEPS):
         nxt = step + 1
-        last = nxt == STEPS
         wait_y(step, ends)
         for c in ends:
             finish_y(step, c)
@@ -618,66 +652,53 @@
         finish_corners_y(step)
         wait_x(step)
         finish_x(step)
-        if not last:
-            for x in rim:
-                stress_layer(step, x)
-        flowed = set()
-        if not last:
-            pack_corners(nxt, (True, False))
-            send_corners(nxt, (True, False))
-            for x in (0, 1, rows_x - 2, rows_x - 1):
-                flow_layer(nxt, x)
-                flowed.add(x)
-            for up in (True, False):
-                pack_x_raw(nxt, up)
-                pack_x_flow(nxt, up)
-            send_x(nxt, (0,))
+        if nxt == STEPS:
+            for i, x in enumerate(rim_of(rows_x)):
+                for comp, value in enumerate(at.stress(step, x)):
+                    edge_out[comp, i] = value
         wait_y(step, middle)
         for c in middle:
             finish_y(step, c)
-        if not last:
-            for x in near:
+        if nxt == STEPS:
+            break
+        sides_x = ((range(CH), 0, (0, 1), False), (range(rows_x - 4, rows_x), None, (rows_x - 2, rows_x - 1), True))
+        flowed, stressed = set(), set()
+        for layers, c, flows, up in sides_x:
+            for x in layers:
                 stress_layer(step, x)
-            for c in ends:
+                stressed.add(x)
+            if c is not None:
                 pack_y_raw(nxt, c)
-            send_y(nxt, ends, (0,))
-            for c in ends:
-                for x in range(c * CH, (c + 1) * CH):
-                    if x not in flowed:
-                        flow_layer(nxt, x)
-                pack_y_flow(nxt, c)
-            send_y(nxt, ends, (1,))
-            send_x(nxt, (1,))
-        if not last:
-            for x in inner:
-                stress_layer(step, x)
-            for c in middle:
-                pack_y_raw(nxt, c)
-            send_y(nxt, middle, (0,))
-            for c in middle:
-                for x in range(c * CH, (c + 1) * CH):
-                    flow_layer(nxt, x)
-                pack_y_flow(nxt, c)
-                send_y(nxt, (c,), (1,))
-
-    for step in range(STEPS):
-        for up in (True, False):
-
-            @pl.when(to_x(up)[0])
-            def _():
-                x_copy(step, up).wait_send()
-
-            @pl.when(to_y(up)[0])
-            def _():
-                for c in range(chunks):
-                    for part in y_parts(step):
-                        y_copy(step, up, c, part).wait_send()
-
-        for d, (cx, cy) in enumerate(CORNERS):
-
-            @pl.when(to_corner(cx, cy)[0])
-            def _():
-                d_copy(step, d).wait_send()
+                send_y(nxt, (c,), (0,))
+            for x in flows:
+                flow_layer(nxt, x)
+                flowed.add(x)
+            pack_corners(nxt, (up,))
+            send_corners(nxt, (up,))
+            pack_x_raw(nxt, up)
+            pack_x_flow(nxt, up)
+            send_x(nxt, (0,), (up,))
+        for x in range(rows_x - CH, rows_x - 4):
+            stress_layer(step, x)
+            stressed.add(x)
+        pack_y_raw(nxt, chunks - 1)
+        send_y(nxt, (chunks - 1,), (0,))
+        for x in (CH, CH + 1, rows_x - CH - 2, rows_x - CH - 1):
+            stress_layer(step, x)
+            stressed.add(x)
+        for c in ends:
+            flow_rest(nxt, c, flowed)
+        send_x(nxt, (1,), (False, True))
+        for c in middle:
+            for x in range(c * CH, (c + 1) * CH):
+                if x not in stressed:
+                    stress_layer(step, x)
+            pack_y_raw(nxt, c)
+            send_y(nxt, (c,), (0,))
+        for c in middle:
+            flow_rest(nxt, c, ())
+        for done in range(STEPS):
+            finish_sends(done)
 
 
 def on_device(nx, ny, velocity, stress, lame_first, modulus, buoyancy, zone, eligible, cohesion, friction, source_cell, source_moment):
@@ -700,6 +721,7 @@
         pltpu.VMEM((6,) + grid, f32),
         pltpu.VMEM(grid, f32),
         pltpu.VMEM(grid, f32),
+        pltpu.VMEM((6, len(rim_of(rows_x)), rows_y, depth), f32),
     ]
     held = pl.pallas_call(
         functools.partial(kernel, nx, ny),
@@ -743,7 +765,7 @@
         out_shape=(jax.ShapeDtypeStruct((3,) + grid, f32), jax.ShapeDtypeStruct((6,) + grid, f32)),
         in_specs=[vmem] * len(fields),
         out_specs=(any_spec, any_spec),
-        scratch_shapes=[pltpu.VMEM((3,) + grid, f32), pltpu.VMEM((6,) + grid, f32), dma((chunks, 2))],
+        scratch_shapes=[pltpu.VMEM((3,) + grid, f32), pltpu.VMEM((6,) + grid, f32), dma((2 + 2 * chunks,))],
         compiler_params=pltpu.CompilerParams(vmem_limit_bytes=24 * 2**20),
     )(*held)
 

time: 15.3 us -> 15.1 us (0.987)
  the two profiles are of different devices: /device:TPU:21 before, /device:TPU:1 now
where the time goes in v5:
time: 15.1 us; the launch traced here: 15 us
  Pallas kernels  14.4 us (95%)
  between operations  0.64 us (4%)
    pallas_call x1, Pallas kernels, on_device(): pl.pallas_call(functools.partial(kernel, nx, ny), out_shape=fields, in_sp...  13.1 us
    pallas_call x1, Pallas kernels, on_device(): pl.pallas_call(finish_kernel, out_shape=(jax.ShapeDtypeStruct((3,) + grid...  1.25 us

profile of v5, /device:TPU:1, one launch (start us, length us, event | category | flops | bytes accessed | tf_op | source)
XLA Modules:
  0.0 15.0 jit_solution(14620477067940826179)
XLA Ops:
  0.6 13.1 %shard_map.122 = (f32[864,128]{1,0:T(8,128)S(1)}, f32[1600,128]{1,0:T(8,128)S(1)}, f32[256,128]{1,0:T(8,128)S(1)}, f32[1776,128]{1,0:T(8,128)S(1)}, f32[32,8,128...) custom-call(f32[768,128]{1,0:T(8,128)} %bitcast.5, ...), custom_call_target="tpu_custom_call" | custom-call | tf_op jit(solution)/shard_map/pallas_call | solution.py:726
  13.7 1.3 %shard_map.123 = (f32[3,32,8,128]{3,2,1,0:T(8,128)}, f32[6,32,8,128]{3,2,1,0:T(8,128)}) custom-call(f32[864,128]{1,0:T(8,128)S(1)} %get-tuple-element.12.sx, f32[1600,128]{1,0:T(8,128)S(1)} %get-tuple-element.13.sy, f32[256,128]{1,0:T(8,128)S(1)} %get-tuple-element.14.zb, f32[1776,128]{1,0:T(8,128)S(1)} %get-tuple-element.15.vb, ...), custom_call_target="tpu_custom_call" | custom-call | tf_op jit(solution)/shard_map/pallas_call | solution.py:763

commit v6 on v5

--- a/solution.py
+++ b/solution.py
@@ -191,7 +191,7 @@
     sx1, sy1, zb1, vb1, lam, mod, inj, cc, cf, edge_out,
     sx0, sy0, zb0, vb0, stage, vel, buo, zone, elig,
     xs, rx, ys, ry, ds, rd, xf, yf, coh_ref, fri_ref, cell_ref, moment_ref,
-    load_sem, xsend, xrecv, ysend, yrecv, dsend, drecv,
+    load_sem, xsend, xrecv, ysend, yrecv, dsend, drecv, ready,
 ):
     rows_x = lam.shape[0]
     rows_y = lam.shape[1]
@@ -214,7 +214,7 @@
         there = jnp.logical_and(to_x(cx)[0], to_y(cy)[0])
         return there, (to_x(cx)[1][0], to_y(cy)[1][1])
 
-    sides = [to_x(True), to_x(False), to_y(True), to_y(False)] + [to_corner(*c) for c in CORNERS]
+    sides = [to_x(True), to_x(False), to_y(True), to_y(False)]
     barrier = pltpu.get_barrier_semaphore()
     for there, target in sides:
 
@@ -559,7 +559,12 @@
         pack_x_flow(0, up)
     heard = sum(there.astype(jnp.int32) for there, _ in sides)
     pl.semaphore_wait(barrier, heard)
-    send_corners(0, (True, False))
+    for there, target in sides:
+
+        @pl.when(there)
+        def _():
+            pl.semaphore_signal(ready, inc=1, device_id=target, device_id_type=MESH)
+
     send_x(0, (0,), (False, True))
     send_y(0, ends, (0,))
     for c in middle:
@@ -580,6 +585,10 @@
     match = row == plane_row
     at_z = (lax.broadcasted_iota(jnp.int32, (depth, cell.shape[1]), 0) == cell_z).astype(jnp.float32)
     for comp in range(6):
+        if comp == 4:
+            pl.semaphore_wait(ready, heard)
+            send_corners(0, (True, False))
+            send_x(0, (1,), (False, True))
         moment = time_step * moment_ref[pl.ds(comp, 1), :]
         value = lax.dot_general(
             jnp.where(match, moment, 0.0),
@@ -590,7 +599,6 @@
         )
         inj[comp] = value.reshape(rows_x, rows_y, depth)
 
-    send_x(0, (1,), (False, True))
     for copy in loads[sources:third]:
         copy.wait()
     frictions, cohesions = [], []
@@ -661,38 +669,34 @@
             finish_y(step, c)
         if nxt == STEPS:
             break
-        sides_x = ((range(CH), 0, (0, 1), False), (range(rows_x - 4, rows_x), None, (rows_x - 2, rows_x - 1), True))
-        flowed, stressed = set(), set()
-        for layers, c, flows, up in sides_x:
+        stressed = set()
+
+        def stress_layers(layers):
             for x in layers:
-                stress_layer(step, x)
-                stressed.add(x)
-            if c is not None:
-                pack_y_raw(nxt, c)
-                send_y(nxt, (c,), (0,))
-            for x in flows:
-                flow_layer(nxt, x)
-                flowed.add(x)
-            pack_corners(nxt, (up,))
-            send_corners(nxt, (up,))
+                if x not in stressed:
+                    stress_layer(step, x)
+                    stressed.add(x)
+
+        stress_layers(rim_of(rows_x))
+        pack_corners(nxt, (False, True))
+        send_corners(nxt, (False, True))
+        flowed = (0, 1, rows_x - 2, rows_x - 1)
+        for x in flowed:
+            flow_layer(nxt, x)
+        for up in (False, True):
             pack_x_raw(nxt, up)
             pack_x_flow(nxt, up)
-            send_x(nxt, (0,), (up,))
-        for x in range(rows_x - CH, rows_x - 4):
-            stress_layer(step, x)
-            stressed.add(x)
-        pack_y_raw(nxt, chunks - 1)
-        send_y(nxt, (chunks - 1,), (0,))
-        for x in (CH, CH + 1, rows_x - CH - 2, rows_x - CH - 1):
-            stress_layer(step, x)
-            stressed.add(x)
+        send_x(nxt, (0,), (False, True))
+        for c in ends:
+            stress_layers(range(c * CH, (c + 1) * CH))
+            pack_y_raw(nxt, c)
+            send_y(nxt, (c,), (0,))
+        stress_layers((CH, CH + 1, rows_x - CH - 2, rows_x - CH - 1))
         for c in ends:
             flow_rest(nxt, c, flowed)
         send_x(nxt, (1,), (False, True))
         for c in middle:
-            for x in range(c * CH, (c + 1) * CH):
-                if x not in stressed:
-                    stress_layer(step, x)
+            stress_layers(range(c * CH, (c + 1) * CH))
             pack_y_raw(nxt, c)
             send_y(nxt, (c,), (0,))
         for c in middle:
@@ -753,6 +757,7 @@
             dma((STEPS, 2, chunks, 2)),
             dma((STEPS, 4)),
             dma((STEPS, 4)),
+            pltpu.SemaphoreType.REGULAR,
         ],
         compiler_params=pltpu.CompilerParams(collective_id=0, has_side_effects=True, vmem_limit_bytes=63_000_000),
     )(

time: 15.1 us -> 15.6 us (1.033)
  Pallas kernels: 14.4 us -> 14.8 us
    pallas_call x1, Pallas kernels: 13.1 us -> 13.6 us  [on_device(): pl.pallas_call(functools.partial(kernel, nx, ny), out_shape=fields, in_sp...]
where the time goes in v6:
time: 15.6 us; the launch traced here: 15.5 us
  Pallas kernels  14.8 us (95%)
  between operations  0.64 us (4%)
    pallas_call x1, Pallas kernels, on_device(): pl.pallas_call(functools.partial(kernel, nx, ny), out_shape=fields, in_sp...  13.6 us
    pallas_call x1, Pallas kernels, on_device(): pl.pallas_call(finish_kernel, out_shape=(jax.ShapeDtypeStruct((3,) + grid...  1.25 us

profile of v6, /device:TPU:1, one launch (start us, length us, event | category | flops | bytes accessed | tf_op | source)
XLA Modules:
  0.0 15.5 jit_solution(11658355520762020851)
XLA Ops:
  0.6 13.6 %shard_map.122 = (f32[864,128]{1,0:T(8,128)S(1)}, f32[1600,128]{1,0:T(8,128)S(1)}, f32[256,128]{1,0:T(8,128)S(1)}, f32[1776,128]{1,0:T(8,128)S(1)}, f32[32,8,128...) custom-call(f32[768,128]{1,0:T(8,128)} %bitcast.5, ...), custom_call_target="tpu_custom_call" | custom-call | tf_op jit(solution)/shard_map/pallas_call | solution.py:730
  14.2 1.3 %shard_map.123 = (f32[3,32,8,128]{3,2,1,0:T(8,128)}, f32[6,32,8,128]{3,2,1,0:T(8,128)}) custom-call(f32[864,128]{1,0:T(8,128)S(1)} %get-tuple-element.12.sx, f32[1600,128]{1,0:T(8,128)S(1)} %get-tuple-element.13.sy, f32[256,128]{1,0:T(8,128)S(1)} %get-tuple-element.14.zb, f32[1776,128]{1,0:T(8,128)S(1)} %get-tuple-element.15.vb, ...), custom_call_target="tpu_custom_call" | custom-call | tf_op jit(solution)/shard_map/pallas_call | solution.py:768

commit v7 on v6

--- a/solution.py
+++ b/solution.py
@@ -215,8 +215,12 @@
         return there, (to_x(cx)[1][0], to_y(cy)[1][1])
 
     sides = [to_x(True), to_x(False), to_y(True), to_y(False)]
+    odd = iy % 2 == 1
+    even = jnp.logical_not(odd)
+    greeted = sides + [(jnp.logical_and(there, odd), target) for there, target in (to_corner(*c) for c in CORNERS)]
+    expected = sides + [(jnp.logical_and(to_corner(*c)[0], even), None) for c in CORNERS]
     barrier = pltpu.get_barrier_semaphore()
-    for there, target in sides:
+    for there, target in greeted:
 
         @pl.when(there)
         def _():
@@ -397,11 +401,13 @@
                     for part in parts:
                         y_copy(step, up, c, part).start()
 
-    def send_corners(step, cxs):
+    def send_corners(step, cxs, when=None):
         for d, (cx, cy) in enumerate(CORNERS):
             if cx in cxs:
 
-                @pl.when(to_corner(cx, cy)[0])
+                there = to_corner(cx, cy)[0]
+
+                @pl.when(there if when is None else jnp.logical_and(there, when))
                 def _():
                     d_copy(step, d).start()
 
@@ -557,14 +563,14 @@
         flow_chunk(c)
     for up in (True, False):
         pack_x_flow(0, up)
-    heard = sum(there.astype(jnp.int32) for there, _ in sides)
-    pl.semaphore_wait(barrier, heard)
-    for there, target in sides:
-
-        @pl.when(there)
+    pl.semaphore_wait(barrier, sum(there.astype(jnp.int32) for there, _ in expected))
+    for i, (there, target) in enumerate(sides):
+
+        @pl.when(jnp.logical_and(there, odd if i < 2 else even))
         def _():
             pl.semaphore_signal(ready, inc=1, device_id=target, device_id_type=MESH)
 
+    send_corners(0, (True, False), even)
     send_x(0, (0,), (False, True))
     send_y(0, ends, (0,))
     for c in middle:
@@ -586,9 +592,13 @@
     at_z = (lax.broadcasted_iota(jnp.int32, (depth, cell.shape[1]), 0) == cell_z).astype(jnp.float32)
     for comp in range(6):
         if comp == 4:
-            pl.semaphore_wait(ready, heard)
-            send_corners(0, (True, False))
             send_x(0, (1,), (False, True))
+
+            @pl.when(odd)
+            def _():
+                pl.semaphore_wait(ready, sum(there.astype(jnp.int32) for there, _ in sides))
+
+            send_corners(0, (True, False), odd)
         moment = time_step * moment_ref[pl.ds(comp, 1), :]
         value = lax.dot_general(
             jnp.where(match, moment, 0.0),

time: 15.6 us -> 16.4 us (1.051)
  Pallas kernels: 14.8 us -> 15.6 us
    pallas_call x1, Pallas kernels: 13.6 us -> 14.4 us  [on_device(): pl.pallas_call(functools.partial(kernel, nx, ny), out_shape=fields, in_sp...]
where the time goes in v7:
time: 16.4 us; the launch traced here: 16.3 us
  Pallas kernels  15.6 us (95%)
  between operations  0.64 us (4%)
    pallas_call x1, Pallas kernels, on_device(): pl.pallas_call(functools.partial(kernel, nx, ny), out_shape=fields, in_sp...  14.4 us
    pallas_call x1, Pallas kernels, on_device(): pl.pallas_call(finish_kernel, out_shape=(jax.ShapeDtypeStruct((3,) + grid...  1.25 us

profile of v7, /device:TPU:1, one launch (start us, length us, event | category | flops | bytes accessed | tf_op | source)
XLA Modules:
  0.0 16.3 jit_solution(18212974446985861430)
XLA Ops:
  0.6 14.4 %shard_map.122 = (f32[864,128]{1,0:T(8,128)S(1)}, f32[1600,128]{1,0:T(8,128)S(1)}, f32[256,128]{1,0:T(8,128)S(1)}, f32[1776,128]{1,0:T(8,128)S(1)}, f32[32,8,128...) custom-call(f32[768,128]{1,0:T(8,128)} %bitcast.5, ...), custom_call_target="tpu_custom_call" | custom-call | tf_op jit(solution)/shard_map/pallas_call | solution.py:740
  15.0 1.3 %shard_map.123 = (f32[3,32,8,128]{3,2,1,0:T(8,128)}, f32[6,32,8,128]{3,2,1,0:T(8,128)}) custom-call(f32[864,128]{1,0:T(8,128)S(1)} %get-tuple-element.12.sx, f32[1600,128]{1,0:T(8,128)S(1)} %get-tuple-element.13.sy, f32[256,128]{1,0:T(8,128)S(1)} %get-tuple-element.14.zb, f32[1776,128]{1,0:T(8,128)S(1)} %get-tuple-element.15.vb, ...), custom_call_target="tpu_custom_call" | custom-call | tf_op jit(solution)/shard_map/pallas_call | solution.py:778

commit v8 on v6

--- a/solution.py
+++ b/solution.py
@@ -191,7 +191,7 @@
     sx1, sy1, zb1, vb1, lam, mod, inj, cc, cf, edge_out,
     sx0, sy0, zb0, vb0, stage, vel, buo, zone, elig,
     xs, rx, ys, ry, ds, rd, xf, yf, coh_ref, fri_ref, cell_ref, moment_ref,
-    load_sem, xsend, xrecv, ysend, yrecv, dsend, drecv, ready,
+    load_sem, xsend, xrecv, ysend, yrecv, dsend, drecv,
 ):
     rows_x = lam.shape[0]
     rows_y = lam.shape[1]
@@ -214,7 +214,7 @@
         there = jnp.logical_and(to_x(cx)[0], to_y(cy)[0])
         return there, (to_x(cx)[1][0], to_y(cy)[1][1])
 
-    sides = [to_x(True), to_x(False), to_y(True), to_y(False)]
+    sides = [to_x(True), to_x(False), to_y(True), to_y(False)] + [to_corner(*c) for c in CORNERS]
     barrier = pltpu.get_barrier_semaphore()
     for there, target in sides:
 
@@ -559,12 +559,7 @@
         pack_x_flow(0, up)
     heard = sum(there.astype(jnp.int32) for there, _ in sides)
     pl.semaphore_wait(barrier, heard)
-    for there, target in sides:
-
-        @pl.when(there)
-        def _():
-            pl.semaphore_signal(ready, inc=1, device_id=target, device_id_type=MESH)
-
+    send_corners(0, (True, False))
     send_x(0, (0,), (False, True))
     send_y(0, ends, (0,))
     for c in middle:
@@ -585,10 +580,6 @@
     match = row == plane_row
     at_z = (lax.broadcasted_iota(jnp.int32, (depth, cell.shape[1]), 0) == cell_z).astype(jnp.float32)
     for comp in range(6):
-        if comp == 4:
-            pl.semaphore_wait(ready, heard)
-            send_corners(0, (True, False))
-            send_x(0, (1,), (False, True))
         moment = time_step * moment_ref[pl.ds(comp, 1), :]
         value = lax.dot_general(
             jnp.where(match, moment, 0.0),
@@ -599,6 +590,7 @@
         )
         inj[comp] = value.reshape(rows_x, rows_y, depth)
 
+    send_x(0, (1,), (False, True))
     for copy in loads[sources:third]:
         copy.wait()
     frictions, cohesions = [], []
@@ -757,7 +749,6 @@
             dma((STEPS, 2, chunks, 2)),
             dma((STEPS, 4)),
             dma((STEPS, 4)),
-            pltpu.SemaphoreType.REGULAR,
         ],
         compiler_params=pltpu.CompilerParams(collective_id=0, has_side_effects=True, vmem_limit_bytes=63_000_000),
     )(

time: 15.6 us -> 15.1 us (0.968)
  Pallas kernels: 14.8 us -> 14.3 us
    pallas_call x1, Pallas kernels: 13.6 us -> 13.1 us  [on_device(): pl.pallas_call(functools.partial(kernel, nx, ny), out_shape=fields, in_sp...]
where the time goes in v8:
time: 15.1 us; the launch traced here: 15 us
  Pallas kernels  14.3 us (95%)
  between operations  0.64 us (4%)
    pallas_call x1, Pallas kernels, on_device(): pl.pallas_call(functools.partial(kernel, nx, ny), out_shape=fields, in_sp...  13.1 us
    pallas_call x1, Pallas kernels, on_device(): pl.pallas_call(finish_kernel, out_shape=(jax.ShapeDtypeStruct((3,) + grid...  1.25 us

profile of v8, /device:TPU:1, one launch (start us, length us, event | category | flops | bytes accessed | tf_op | source)
XLA Modules:
  0.0 15.0 jit_solution(13200900076807791209)
XLA Ops:
  0.6 13.1 %shard_map.122 = (f32[864,128]{1,0:T(8,128)S(1)}, f32[1600,128]{1,0:T(8,128)S(1)}, f32[256,128]{1,0:T(8,128)S(1)}, f32[1776,128]{1,0:T(8,128)S(1)}, f32[32,8,128...) custom-call(f32[768,128]{1,0:T(8,128)} %bitcast.5, ...), custom_call_target="tpu_custom_call" | custom-call | tf_op jit(solution)/shard_map/pallas_call | solution.py:722
  13.7 1.3 %shard_map.123 = (f32[3,32,8,128]{3,2,1,0:T(8,128)}, f32[6,32,8,128]{3,2,1,0:T(8,128)}) custom-call(f32[864,128]{1,0:T(8,128)S(1)} %get-tuple-element.12.sx, f32[1600,128]{1,0:T(8,128)S(1)} %get-tuple-element.13.sy, f32[256,128]{1,0:T(8,128)S(1)} %get-tuple-element.14.zb, f32[1776,128]{1,0:T(8,128)S(1)} %get-tuple-element.15.vb, ...), custom_call_target="tpu_custom_call" | custom-call | tf_op jit(solution)/shard_map/pallas_call | solution.py:759
